TPU v7x, 32 devices: a whole 2x2x4 slice. The times are simulated.
32 devices in a mesh: src: 4 (over y, x), snk: 8 (over z, core).
Axes of the slice: x: 2, y: 2, z: 4, core: 2. Of those that a mesh axis runs over, the one named last changes fastest.
Arguments:
- perambulator: bfloat16 [4, 8, 2, 1024, 1024], P('src', 'snk'), may hold values from -0.25976562 to 0.25976562
- elementals: bfloat16 [8, 4, 2, 256, 256], P('snk', None, None, 'src'), may hold values from -0.25 to 0.25
- momentum: int32 [8], P('snk'), may hold values from 0 to 3
- routes: int32 [4, 8, 16, 1], P('src'), may hold values from 0 to 7; in each aligned block of 16 rows (0 to 15, 16 to 31, ..., all dimensions but the last counted through in order) at most 4 rows name the same one
- node_of: int32 [4, 8, 16], P('src'), may hold values from 0 to 7
- owner_slot: int32 [8], replicated, may hold values from 0 to 7, each once
Outputs:
- nodes: float32 [8, 2, 64, 1024], P('snk', None, 'src')
Inputs may be any that keep to these rules, and one draw needn't show every extreme that they name: `routes`: among the 16 slabs of one tile (one s and k), at most 4 name the same sink timeslice. `owner_slot`: each value appears exactly once.
All inputs are finite; a program needn't handle non-finite values.
Results may differ from a plain program's by a relative error of at most 0.005.
Values may be sent and summed in bfloat16 or wider, within the bound.
No kernel may reach another device: no remote copies, remote signals or barrier semaphores. Data moves between devices by JAX's collectives and lax.ppermute only.
A program may use at most 128 MiB of HBM per device.

v0:
```python
import jax
import jax.numpy as jnp
from jax import lax
from jax.sharding import PartitionSpec as P

RB = 64


def on_device(perambulator, elementals, momentum, routes, node_of, owner_slot):
    source_tile = perambulator[0, 0]
    order = source_tile.shape[1]
    eigen = elementals.shape[-1]
    right = source_tile.reshape(2, eigen, -1)
    sink_count = lax.axis_size("snk")
    myself = lax.axis_index("snk")
    slab_rows = RB
    slab_count = order // slab_rows
    capacity = max(2, 2 * slab_count // sink_count)
    node_count = owner_slot.shape[0]
    chosen = momentum[0]
    piece = lax.dynamic_index_in_dim(
        lax.all_gather(elementals[0], "src", axis=2, tiled=True), chosen, 0, False
    )
    real_part = jnp.dot(piece[0], right[0], preferred_element_type=jnp.float32) - jnp.dot(
        piece[1], right[1], preferred_element_type=jnp.float32
    )
    imag_part = jnp.dot(piece[0], right[1], preferred_element_type=jnp.float32) + jnp.dot(
        piece[1], right[0], preferred_element_type=jnp.float32
    )
    dressed = jnp.stack([real_part, imag_part]).astype(jnp.bfloat16)
    own_tile = dressed.reshape(2, order, order)
    slabs = dressed.reshape(2, slab_count, slab_rows, order)
    route_table = routes[0, :, :, 0]
    blocks = jnp.arange(slab_count, dtype=jnp.int32)
    earlier = blocks[None, :] < blocks[:, None]
    matching = route_table[:, :, None] == route_table[:, None, :]
    ordinal = jnp.sum(jnp.logical_and(matching, earlier[None]), axis=2)
    sink_ids = jnp.arange(sink_count, dtype=jnp.int32)
    slot_ids = jnp.arange(capacity, dtype=jnp.int32)
    selection = jnp.logical_and(
        route_table[:, None, None, :] == sink_ids[None, :, None, None],
        ordinal[:, None, None, :] == slot_ids[None, None, :, None],
    )
    outgoing = lax.dynamic_index_in_dim(selection, myself, 0, False).astype(jnp.bfloat16)
    packed = jnp.einsum(
        "hcb,xbrm->hcxrm", outgoing, slabs, preferred_element_type=jnp.float32
    ).astype(jnp.bfloat16)
    arrived = lax.all_to_all(packed, "snk", split_axis=0, concat_axis=0, tiled=True)
    first = arrived[:, :, 0]
    second = arrived[:, :, 1]
    real_part = jnp.einsum(
        "kirm,jm->kirj", first, own_tile[0], preferred_element_type=jnp.float32
    ) + jnp.einsum("kirm,jm->kirj", second, own_tile[1], preferred_element_type=jnp.float32)
    imag_part = jnp.einsum(
        "kirm,jm->kirj", second, own_tile[0], preferred_element_type=jnp.float32
    ) - jnp.einsum("kirm,jm->kirj", first, own_tile[1], preferred_element_type=jnp.float32)
    products = jnp.stack([real_part, imag_part], axis=2)
    incoming = lax.dynamic_index_in_dim(selection, myself, 1, False).astype(jnp.float32)
    node_ids = jnp.arange(node_count, dtype=jnp.int32)
    node_match = (node_of[0][:, :, None] == node_ids[None, None, :]).astype(jnp.int32)
    position = jnp.sum(node_match * owner_slot[None, None, :], axis=2)
    placed = (position[:, :, None] == node_ids[None, None, :]).astype(jnp.float32)
    weights = jnp.einsum("kcb,kbn->nkc", incoming, placed)
    whole = jnp.einsum(
        "nkc,kcxrm->nxrm",
        weights,
        products,
        precision=lax.Precision.HIGHEST,
        preferred_element_type=jnp.float32,
    )
    summed_rows = lax.psum_scatter(whole, "src", scatter_dimension=2, tiled=True)
    return lax.psum_scatter(summed_rows, "snk", scatter_dimension=0, tiled=True)


def solution(mesh):
    placed = (
        P("src", "snk", None, None, None),
        P("snk", None, None, "src", None),
        P("snk"),
        P("src", None, None, None),
        P("src", None, None),
        P(),
    )
    return jax.shard_map(
        on_device,
        mesh=mesh,
        in_specs=placed,
        out_specs=P("snk", None, "src", None),
        check_vma=False,
    )
```

profile of v0, /device:TPU:0, one launch (start us, length us, event | category | flops | bytes accessed | tf_op | source)
XLA Modules:
  0.0 428.5 jit_solution(4687263833813959302)
XLA Ops:
  7.9 4.0 fusion.24
  11.9 2.5 squeeze.51
  14.4 3.1 squeeze.53
  18.0 20.5 %all-gather.3.cloned.1.call-done = bf16[1,4,2,256,256]{4,3,2,1,0:T(8,128)(2,1)} async-done(((bf16[1,4,2,64,256]{4,3,2,1,0:T(8,128)(2,1)}), bf16[1,4,2,256,256]{4,3,2,1,0:T(8,128)(2,1)}) %all-gather.3.cloned.1.call-update) | async-done | bytes 1048592 | tf_op jit(solution)/shard_map/all_gather | solution.py:22
  40.3 2.7 fusion.18
  45.0 4.4 %stack.22 = bf16[1,16,64,1024]{3,2,1,0:T(8,128)(2,1)} reshape(bf16[256,4096]{1,0:T(8,128)(2,1)} %fusion.3) | data formatting | bytes 4194304 | tf_op jit(solution)/shard_map/stack | solution.py:30
  49.5 4.2 copy.37
  53.7 2.1 fusion.2
  55.8 3.1 stack.21
  60.5 4.6 %convolution_convert_fusion = bf16[8,4,2,64,1024]{4,0,3,2,1:T(8,128)(2,1)} fusion(bf16[1,16,64,1024]{3,1,2,0:T(8,128)(2,1)S(1)} %copy-done.3, bf16[1,16,64,1024]{3,1,2,0:T(8,128)(2,1)S(1)} %copy.36, pred[1,8,4,16]{3,0,2,1:T(4,128)(4,1)S(1)} %constant_dynamic-slice_fusion), kind=kOutput, calls=%fused_computation.5 | convolution fusion | flops 146800640 | bytes 12583424 | tf_op jit(solution)/shard_map/hcb,xbrm->hcxrm/dot_general | solution.py:45
  65.0 11.3 %copy.38 = bf16[8,4,2,64,1024]{4,3,2,1,0:T(8,128)(2,1)} copy(bf16[8,4,2,64,1024]{4,0,3,2,1:T(8,128)(2,1)} %convolution_convert_fusion) | data formatting | bytes 16777216 | tf_op jit(solution)/shard_map/convert_element_type | solution.py:47
  76.4 5.1 %all-to-all-start = ((bf16[8,4,2,64,1024]{4,3,2,1,0:T(8,128)(2,1)}), bf16[8,4,2,64,1024]{4,3,2,1,0:T(8,128)(2,1)}, u32[]{:S(2)}, u32[]{:S(2)}) async-start(bf16[8,4,2,64,1024]{4,3,2,1,0:T(8,128)(2,1)} %copy.38), calls=%async_computation | async-start | bytes 16777216 | tf_op jit(solution)/shard_map/all_to_all | solution.py:48
  81.7 2.8 reshape.60
  84.5 4.5 %reshape.59 = bf16[1024,1024,1,1]{1,0,2,3:T(8,128)(2,1)} reshape(bf16[256,4096]{1,0:T(8,128)(2,1)} %fusion.2) | data formatting | bytes 4194304 | tf_op jit(solution)/shard_map/squeeze | solution.py:52
  89.0 176.3 %all-to-all-done = bf16[8,4,2,64,1024]{4,3,2,1,0:T(8,128)(2,1)} async-done(((bf16[8,4,2,64,1024]{4,3,2,1,0:T(8,128)(2,1)}), bf16[8,4,2,64,1024]{4,3,2,1,0:T(8,128)(2,1)}, u32[]{:S(2)}, u32[]{:S(2)}) %all-to-all-start) | async-done | bytes 8388640 | tf_op jit(solution)/shard_map/all_to_all | solution.py:48
  265.3 6.5 %fusion.6 = f32[8,4,64,1024]{3,2,1,0:T(8,128)S(1)} fusion(bf16[8,4,2,64,1024]{4,3,2,1,0:T(8,128)(2,1)} %all-to-all-done, bf16[1024,1024,1,1]{1,0,2,3:T(8,128)(2,1)S(1)} %copy-done.4), kind=kOutput, calls=%fused_computation.15 | convolution fusion | flops 4294967296 | bytes 14680064 | tf_op jit(solution)/shard_map/kirm,jm->kirj/dot_general | solution.py:56
  271.9 9.0 %fusion.7 = f32[8,4,64,1024]{3,2,1,0:T(8,128)} fusion(bf16[8,4,2,64,1024]{4,3,2,1,0:T(8,128)(2,1)} %all-to-all-done, bf16[1024,1024,1,1]{1,0,2,3:T(8,128)(2,1)S(1)} %copy-done.5), kind=kOutput, calls=%fused_computation.16 | convolution fusion | flops 4294967296 | bytes 14680064 | tf_op jit(solution)/shard_map/kirm,jm->kirj/dot_general | solution.py:51
  280.9 6.4 %subtract_bitcast_fusion = f32[8,4,1,64,1024]{4,3,1,0,2:T(8,128)S(1)} fusion(f32[8,4,64,1024]{3,2,1,0:T(8,128)S(1)} %fusion.6, bf16[8,4,2,64,1024]{4,3,2,1,0:T(8,128)(2,1)} %all-to-all-done, bf16[1024,1024,1,1]{1,0,2,3:T(8,128)(2,1)S(1)} %copy-done.5), kind=kOutput, calls=%fused_computation.3 | convolution fusion | flops 4297064448 | bytes 23068672 | tf_op jit(solution)/shard_map/kirm,jm->kirj/dot_general | solution.py:54
  287.2 10.9 %add_bitcast_fusion = f32[8,4,1,64,1024]{4,3,1,0,2:T(8,128)S(1)} fusion(f32[8,4,64,1024]{3,2,1,0:T(8,128)} %fusion.7, bf16[8,4,2,64,1024]{4,3,2,1,0:T(8,128)(2,1)} %all-to-all-done, bf16[1024,1024,1,1]{1,0,2,3:T(8,128)(2,1)S(1)} %copy-done.4), kind=kOutput, calls=%fused_computation.4 | convolution fusion | flops 4297064448 | bytes 23068672 | tf_op jit(solution)/shard_map/kirm,jm->kirj/dot_general | solution.py:53
  298.1 2.4 pad_maximum_fusion
  300.5 29.9 %fusion.10 = f32[8,2,64,1024]{3,0,2,1:T(8,128)S(1)} fusion(f32[8,8,4,1,1]{0,2,1,4,3:T(4,128)S(1)} %convolution_bitcast_fusion, f32[8,4,2,64,1024]{4,3,1,0,2:T(8,128)S(1)} %pad_maximum_fusion), kind=kOutput, calls=%fused_computation.19 | convolution fusion | flops 402653184 | bytes 20972544 | tf_op jit(solution)/shard_map/nkc,kcxrm->nxrm/dot_general | solution.py:64
  330.7 4.3 %copy.53 = f32[8,8,16,1024]{3,1,2,0:T(8,128)} copy(f32[8,8,16,1024]{3,2,1,0:T(8,128)S(1)} %bitcast.89) | data formatting | bytes 8388608
  335.1 50.6 %reduce-scatter.8.cloned.1.call-done = f32[16,16384]{1,0:T(8,128)} async-done(((f32[64,16384]{1,0:T(8,128)}), f32[16,16384]{1,0:T(8,128)}) %reduce-scatter.8.cloned.1.call-update) | async-done | bytes 1048592
  389.2 32.8 %reduce-scatter.6.cloned.1.call-done = f32[1,2,16,1024]{3,2,1,0:T(8,128)} async-done(((f32[8,2,16,1024]{3,2,1,0:T(8,128)}), f32[1,2,16,1024]{3,2,1,0:T(8,128)}) %reduce-scatter.6.cloned.1.call-update) | async-done | bytes 131088 | tf_op jit(solution)/shard_map/reduce_scatter | solution.py:72
  (40 shorter events, 10.6 us)
Async XLA Ops:
  6.5 31.9 %all-gather.3.cloned.1.call-start = ((), (), s32[]{:S(2)}) async-start(), calls=%async_computation.4 | async-start | bytes 1310720 | tf_op jit(solution)/shard_map/all_gather | solution.py:22
  11.9 5.7 %copy-start.6 = (s32[1,8,16,1]{2,3,1,0:T(1,128)S(1)}, s32[1,8,16,1]{2,3,1,0:T(1,128)}, u32[]{:S(2)}) copy-start(s32[1,8,16,1]{2,3,1,0:T(1,128)} %param.9) | copy-start | bytes 1540
  38.4 1.8 copy-start
  49.5 4.2 copy-start.2
  58.9 1.6 copy-start.3
  76.4 5.2 %copy-start.7 = (s32[1,8,16]{2,1,0:T(8,128)S(1)}, s32[1,8,16]{2,1,0:T(8,128)}, u32[]{:S(2)}) copy-start(s32[1,8,16]{2,1,0:T(8,128)} %param.10) | copy-start | bytes 1540
  76.4 5.2 %copy-start.8 = (s32[8]{0:T(128)S(1)}, s32[8]{0:T(128)}, u32[]{:S(2)}) copy-start(s32[8]{0:T(128)} %param.11) | copy-start | bytes 100
  76.4 5.4 %copy-start.1 = (bf16[256,4096]{1,0:T(8,128)(2,1)S(1)}, bf16[256,4096]{1,0:T(8,128)(2,1)}, u32[]{:S(2)}) copy-start(bf16[256,4096]{1,0:T(8,128)(2,1)} %fusion.3) | copy-start | bytes 6291460
  76.4 188.9 %all-to-all-start = ((bf16[8,4,2,64,1024]{4,3,2,1,0:T(8,128)(2,1)}), bf16[8,4,2,64,1024]{4,3,2,1,0:T(8,128)(2,1)}, u32[]{:S(2)}, u32[]{:S(2)}) async-start(bf16[8,4,2,64,1024]{4,3,2,1,0:T(8,128)(2,1)} %copy.38), calls=%async_computation | async-start | bytes 16777216 | tf_op jit(solution)/shard_map/all_to_all | solution.py:48
  81.4 304.3 %reduce-scatter.8.cloned.1.call-start = ((), (), s32[]{:S(2)}) async-start(), calls=%async_computation.5 | async-start | bytes 5242880
  84.5 180.8 %copy-start.4 = (bf16[1024,1024,1,1]{1,0,2,3:T(8,128)(2,1)S(1)}, bf16[1024,1024,1,1]{1,0,2,3:T(8,128)(2,1)}, u32[]{:S(2)}) copy-start(bf16[1024,1024,1,1]{1,0,2,3:T(8,128)(2,1)} %reshape.60) | copy-start | bytes 6291460
  265.3 6.5 %copy-start.5 = (bf16[1024,1024,1,1]{1,0,2,3:T(8,128)(2,1)S(1)}, bf16[1024,1024,1,1]{1,0,2,3:T(8,128)(2,1)}, u32[]{:S(2)}) copy-start(bf16[1024,1024,1,1]{1,0,2,3:T(8,128)(2,1)} %reshape.59) | copy-start | bytes 6291460
  335.1 86.9 %reduce-scatter.6.cloned.1.call-start = ((), (), s32[]{:S(2)}) async-start(), calls=%async_computation.3 | async-start | bytes 1179648 | tf_op jit(solution)/shard_map/reduce_scatter | solution.py:72
Sparse Core Ops, SparseCore 0:
  9.2 29.2 all-gather.2
  335.2 50.5 reduce-scatter.7
  389.3 32.6 reduce-scatter.5
where the time goes:
time: 429 us
  waiting for transfers between devices  281 us (66%)
  matrix products  75 us (17%)
  local copies, waits for them, and re-layouts  50.7 us (12%)
  between operations  14 us (3%)
  starting transfers between devices  5.15 us (1%)
    all_to_all x1, waiting for transfers between devices, on_device(): lax.all_to_all(packed, 'snk', split_axis=0, concat_axis=0, tiled=True)  176 us
    unnamed x4, waiting for transfers between devices  51.4 us
    reduce_scatter x1, waiting for transfers between devices, on_device(): return lax.psum_scatter(summed_rows, 'snk', scatter_dimension=0, tiled=True)  32.8 us
    dot_general x1, matrix products, on_device(): jnp.einsum('nkc,kcxrm->nxrm', weights, products, precision=lax.Precision....  29.9 us
    all_gather x1, waiting for transfers between devices, on_device(): lax.all_gather(elementals[0], 'src', axis=2, tiled=True)  20.5 us
    another operation x4, local copies, waits for them, and re-layouts, on_device(): dressed = jnp.stack([real_part, imag_part]).astype(jnp.bfloat16)  12.9 us
    convert_element_type x1, local copies, waits for them, and re-layouts, on_device(): packed = jnp.einsum('hcb,xbrm->hcxrm', outgoing, slabs, preferred_element...  11.3 us
    dot_general x1, matrix products, on_device(): jnp.einsum('kirm,jm->kirj', second, own_tile[1], preferred_element_type=j...  10.9 us
  transfers between devices with their start and end apart: 4, of which 4 were waited for; matrix products, arithmetic and copies ran while one was open for 4% of the time, Pallas kernels for 0%

commit v1 on v0

v1 whole, which is shorter than its diff:
```python
import functools

import jax
import jax.numpy as jnp
from jax import lax
from jax.experimental import pallas as pl
from jax.experimental.pallas import tpu as pltpu
from jax.sharding import PartitionSpec as P


FINISH_MIB = 40
F32 = jnp.float32
BF16 = jnp.bfloat16
VMEM = pl.BlockSpec(memory_space=pltpu.VMEM)
SMEM = pl.BlockSpec(memory_space=pltpu.SMEM)
ANY = pl.BlockSpec(memory_space=pl.ANY)


def params(mib):
    return pltpu.CompilerParams(vmem_limit_bytes=mib * 1024 * 1024)


def swap(value, axis, size, flip):
    return lax.ppermute(value, axis, [(i, i ^ flip) for i in range(size)])


def cut_kernel(where_ref, tile_hbm, out_ref, sems):
    width = out_ref.shape[-1] // 2
    start = pl.multiple_of(where_ref[0] * width, width)
    copies = [
        pltpu.make_async_copy(
            tile_hbm.at[x, :, pl.ds(start, width)],
            out_ref.at[:, x * width : (x + 1) * width],
            sems.at[x],
        )
        for x in range(2)
    ]
    for copy in copies:
        copy.start()
    for copy in copies:
        copy.wait()


def cut(tile, where, width):
    _, order, _ = tile.shape
    return pl.pallas_call(
        cut_kernel,
        out_shape=jax.ShapeDtypeStruct((order, 2 * width), tile.dtype),
        in_specs=[SMEM, ANY],
        out_specs=VMEM,
        scratch_shapes=[pltpu.SemaphoreType.DMA((2,))],
        compiler_params=params(60),
        cost_estimate=pl.CostEstimate(
            flops=0, bytes_accessed=8 * order * width, transcendentals=0
        ),
        name="cut",
    )(where, tile)


def dress_kernel(spin, pieces, where_ref, phi_ref, tile_ref, *refs):
    refs = list(refs)
    outs = [[refs.pop(0) for _ in range(n)] for n in pieces]
    sems = refs.pop()
    wide_ref = refs.pop()
    rights = refs
    order = wide_ref.shape[0]
    eigen = order // spin
    copies = []
    for j, right_ref in enumerate(rights):
        width = right_ref.shape[1] // 2
        for x in range(2):
            if len(tile_ref.shape) == 3:
                start = pl.multiple_of(where_ref[j] * width, width)
                source = tile_ref.at[x, :, pl.ds(start, width)]
            else:
                source = tile_ref.at[:, x * width : (x + 1) * width]
            target = right_ref.at[:order, x * width : (x + 1) * width]
            copies.append(pltpu.make_async_copy(source, target, sems.at[2 * j + x]))
            copies[-1].start()

    row = lax.broadcasted_iota(jnp.int32, (order, eigen), 0)
    col = lax.broadcasted_iota(jnp.int32, (order, eigen), 1)
    spread = (row // spin == col).astype(BF16)
    r = lax.broadcasted_iota(jnp.int32, (eigen, order), 0)
    c = lax.broadcasted_iota(jnp.int32, (eigen, order), 1)
    same = r % spin == c % spin
    for x in range(2):
        tall = jnp.dot(spread, phi_ref[x], preferred_element_type=F32).astype(BF16)
        for part in range(spin):
            rows = slice(part * eigen, (part + 1) * eigen)
            wide = lax.dot_general(
                tall[rows], spread, (((1,), (1,)), ((), ())), preferred_element_type=F32
            )
            wide_ref[rows, x * order : (x + 1) * order] = jnp.where(same, wide, 0.0).astype(BF16)

    block = 256
    for j, right_ref in enumerate(rights):
        copies[2 * j].wait()
        copies[2 * j + 1].wait()
        width = right_ref.shape[1] // 2
        right_ref[order:, :width] = -right_ref[:order, width:]
        right_ref[order:, width:] = right_ref[:order, :width]

        def multiply(i, carry):
            rows = pl.ds(pl.multiple_of(i * block, block), block)
            both = jnp.dot(
                wide_ref[rows, :], right_ref[...], preferred_element_type=F32
            ).astype(BF16)
            part = width // len(outs[j])
            for k, out_ref in enumerate(outs[j]):
                out_ref[rows, :part] = both[:, k * part : (k + 1) * part]
                out_ref[rows, part:] = both[:, width + k * part : width + (k + 1) * part]
            return carry

        lax.fori_loop(0, order // block, multiply, 0)


def dress(phi, spin, tile, where, widths, pieces):
    order = phi.shape[-1] * spin
    outs = []
    for width, n in zip(widths, pieces):
        outs += [jax.ShapeDtypeStruct((order, 2 * width // n), BF16)] * n
    scratch = [pltpu.VMEM((2 * order, 2 * width), BF16) for width in widths]
    scratch += [
        pltpu.VMEM((order, 2 * order), BF16),
        pltpu.SemaphoreType.DMA((2 * len(widths),)),
    ]
    flat = pl.pallas_call(
        functools.partial(dress_kernel, spin, pieces),
        out_shape=outs,
        in_specs=[SMEM, VMEM, ANY],
        out_specs=[VMEM] * len(outs),
        scratch_shapes=scratch,
        compiler_params=params(58),
        cost_estimate=pl.CostEstimate(
            flops=8 * order * order * sum(widths),
            bytes_accessed=8 * order * sum(widths),
            transcendentals=0,
        ),
        name="dress",
    )(where, phi, tile)
    flat = list(flat)
    return [[flat.pop(0) for _ in range(n)] for n in pieces]


def clear(sums_ref):
    def one(i, carry):
        sums_ref[i] = jnp.zeros(sums_ref.shape[1:], F32)
        return carry

    lax.fori_loop(0, sums_ref.shape[0], one, 0)


def add_slabs(dest_ref, sink, tile_ref, sums_ref, base=0):
    groups, slab_rows, _ = sums_ref.shape

    def one(b, carry):
        dest = dest_ref[sink, b] - base

        @pl.when(jnp.logical_and(dest >= 0, dest < groups))
        def _():
            start = pl.multiple_of(b * slab_rows, slab_rows)
            sums_ref[dest] += tile_ref[pl.ds(start, slab_rows), :].astype(F32)

        return carry

    lax.fori_loop(0, tile_ref.shape[0] // slab_rows, one, 0)


def gather_kernel(count, sinks_ref, dest_ref, *refs):
    sums_ref = refs[count]
    clear(sums_ref)
    for i, tile_ref in enumerate(refs[:count]):
        add_slabs(dest_ref, sinks_ref[i], tile_ref, sums_ref)


def gather(sinks, dest, tiles, groups):
    order, width = tiles[0].shape
    slab_rows = order // dest.shape[1]
    return pl.pallas_call(
        functools.partial(gather_kernel, len(tiles)),
        out_shape=jax.ShapeDtypeStruct((groups, slab_rows, width), F32),
        in_specs=[SMEM, SMEM] + [VMEM] * len(tiles),
        out_specs=VMEM,
        compiler_params=params(24),
        cost_estimate=pl.CostEstimate(
            flops=len(tiles) * order * width,
            bytes_accessed=2 * len(tiles) * order * width + 4 * groups * slab_rows * width,
            transcendentals=0,
        ),
        name="gather",
    )(sinks, dest, *tiles)


def finish_kernel(count, late, nodes, base, first, last, sinks_ref, dest_ref, here_ref, *refs):
    refs = list(refs)
    early_ref = None if late == count else refs.pop(0)
    before_ref = None if first else refs.pop(0)
    tiles = [refs.pop(0) for _ in range(count)]
    total_ref = refs.pop() if last else refs[0]
    left_ref = refs.pop()
    sums_ref = refs.pop()
    outs = refs
    order, width = tiles[0].shape
    half = width // 2
    slab_rows = sums_ref.shape[1]

    groups = sums_ref.shape[0]
    start = base * count
    if early_ref is None:
        clear(sums_ref)
    else:

        def take(i, carry):
            sums_ref[i] = early_ref[start + i]
            return carry

        lax.fori_loop(0, groups, take, 0)
    for i in range(count - late, count):
        add_slabs(dest_ref, sinks_ref[i], tiles[i], sums_ref, start)

    def place(node, carry):
        rows = pl.multiple_of(node * 2 * slab_rows, 2 * slab_rows)
        for i in range(count):
            real = sums_ref[node * count + i, :, :half].astype(BF16)
            imag = sums_ref[node * count + i, :, half:].astype(BF16)
            one = slice(i * width, i * width + half)
            two = slice(i * width + half, (i + 1) * width)
            left_ref[pl.ds(rows, slab_rows), one] = real
            left_ref[pl.ds(rows + slab_rows, slab_rows), one] = imag
            left_ref[pl.ds(rows, slab_rows), two] = imag
            left_ref[pl.ds(rows + slab_rows, slab_rows), two] = -real
        return carry

    lax.fori_loop(0, nodes, place, 0)
    block = 256

    def multiply(j, carry):
        cols = pl.ds(pl.multiple_of(j * block, block), block)
        rows = pl.ds(2 * base, 2 * nodes)
        product = 0.0 if first else before_ref[rows, :, cols].reshape(-1, block)
        for i in range(count):
            product += lax.dot_general(
                left_ref[:, i * width : (i + 1) * width],
                tiles[i][cols, :],
                (((1,), (1,)), ((), ())),
                preferred_element_type=F32,
            )
        total_ref[:, :, cols] = product.reshape(2 * nodes, slab_rows, block)
        return carry

    lax.fori_loop(0, order // block, multiply, 0)
    if last:
        rows = slab_rows // len(outs)
        for u, out_ref in enumerate(outs):
            start = pl.multiple_of((here_ref[0] ^ u) * rows, rows)
            out_ref[...] = total_ref[:, pl.ds(start, rows), :].astype(out_ref.dtype)


def finish(sinks, dest, here, sums, before, tiles, late, nodes, base, parts):
    order, width = tiles[0].shape
    count = len(tiles)
    slab_rows = order // dest.shape[1]
    first, last = before is None, parts > 0
    whole = jax.ShapeDtypeStruct((2 * nodes, slab_rows, order), F32)
    shape = (2 * nodes, slab_rows // max(parts, 1), order)
    outs = [jax.ShapeDtypeStruct(shape, BF16 if u else F32) for u in range(parts)]
    extra = [a for a in (sums, before) if a is not None]
    scratch = [
        pltpu.VMEM((count * nodes, slab_rows, width), F32),
        pltpu.VMEM((2 * nodes * slab_rows, count * width), BF16),
    ]
    if last:
        scratch.append(pltpu.VMEM(whole.shape, F32))
    return pl.pallas_call(
        functools.partial(finish_kernel, count, late, nodes, base, first, last),
        out_shape=outs if last else [whole],
        in_specs=[SMEM, SMEM, SMEM] + [VMEM] * (count + len(extra)),
        out_specs=[VMEM] * max(parts, 1),
        scratch_shapes=scratch,
        compiler_params=params(FINISH_MIB),
        cost_estimate=pl.CostEstimate(
            flops=8 * nodes * slab_rows * order * count * width,
            bytes_accessed=2 * count * order * width,
            transcendentals=0,
        ),
        name="finish",
    )(sinks, dest, here, *extra, *tiles)


def on_device(perambulator, elementals, momentum, routes, node_of, owner_slot):
    tile = perambulator[0, 0]
    order = tile.shape[1]
    eigen = elementals.shape[-1]
    spin = order // eigen
    sink_count = lax.axis_size("snk")
    source_count = lax.axis_size("src")
    chips = sink_count // 2
    width = order // chips
    node_count = owner_slot.shape[0]
    nodes = node_count // 2
    sink = lax.axis_index("snk")
    source = lax.axis_index("src")
    chip, core = sink // 2, sink % 2
    raw = chips // 2
    steps = [t for t in range(1, chips) if t != raw]
    sends = lambda value, t: swap(value, "snk", sink_count, 2 * t)
    column = lambda t: (chip ^ t).astype(jnp.int32).reshape(1)

    route = routes[0, :, :, 0]
    node_ids = jnp.arange(node_count, dtype=jnp.int32)
    match = (node_of[0][:, :, None] == node_ids).astype(jnp.int32)
    position = jnp.sum(match * owner_slot, axis=2)
    partner = 2 * ((route // 2) ^ chip) + ((route % 2) ^ core)

    chunks = 2 if width % 256 == 0 else 1
    part = width // chunks
    tie = lax.optimization_barrier

    first = cut(tile, column(raw) * chunks, part)
    far_raw = sends(first, raw)
    piece = lax.dynamic_index_in_dim(elementals[0], momentum[0], 0, False)
    piece, first = tie((piece, first))
    phi = near_phi = lax.all_gather(piece, "src", axis=1, tiled=True)
    own = {}
    (own[steps[-1]],) = dress(phi, spin, tile, column(steps[-1]), [width], [chunks])
    phi, own[steps[-1]] = tie((phi, own[steps[-1]]))
    rest = ([raw] if chunks > 1 else []) + steps[-2::-1] + [0]
    where = [column(t) * chunks + 1 if t == raw else column(t) for t in rest]
    made = dress(
        phi,
        spin,
        tile,
        jnp.concatenate(where),
        [part if t == raw else width for t in rest],
        [1 if t == raw else chunks for t in rest],
    )
    own.update(zip(rest, made))
    if chunks > 1:
        own[raw] = [None] + own[raw]
    piece, near_phi = tie((piece, near_phi))
    far_piece = sends(piece, raw)
    far_phi = lax.all_gather(far_piece, "src", axis=1, tiled=True)

    here = source.astype(jnp.int32).reshape(1)
    arrival = [0, raw] + steps
    sinks = []
    places = []
    for t in arrival:
        sinks += [2 * (chip ^ t) + core, 2 * (chip ^ t) + (1 - core)]
        places += [2 * t, 2 * t + 1]
    sinks = jnp.stack(sinks).astype(jnp.int32)
    rank = jnp.array([places.index(i) for i in range(sink_count)], jnp.int32)
    ids = jnp.arange(sink_count, dtype=jnp.int32)
    order_of = jnp.sum((partner[:, :, None] == ids).astype(jnp.int32) * rank, axis=2)
    slot = ((position // 2) ^ chip) * sink_count + order_of
    dest = jnp.where(position % 2 == core, slot, -1).astype(jnp.int32)

    total = None
    seen = {}
    for c in range(chunks):
        here_now = {0: own[0][c]}
        if c:
            for t in [raw] + steps:
                sent, _ = tie((own[t][c], seen[t]))
                here_now[t] = sends(sent, t)
        else:
            for t in steps[::-1]:
                here_now[t] = seen[t] = sends(own[t][c], t)
            seen[raw] = far_raw
            for t in steps[:-1]:
                seen[t] = own[t][0]
            zero = jnp.zeros((1,), jnp.int32)
            (here_now[raw],) = dress(far_phi, spin, far_raw, zero, [part], [1])[0]
        tiles = []
        for t in arrival:
            tiles += [here_now[t], swap(here_now[t], "snk", sink_count, 1)]
        count = len(tiles)
        if c < chunks - 1:
            (total,) = finish(sinks, dest, here, None, total, tiles, count, nodes, 0, 0)
        else:
            late = 2
            sums = gather(sinks, dest, tiles[: count - late], sink_count * nodes)

    half = nodes // 2
    kept = []
    for base in (half, 0):
        outs = finish(sinks, dest, here, sums, total, tiles, late, half, base, source_count)
        moved = [outs[0]]
        for u in list(range(1, source_count))[::-1]:
            moved.append(swap(outs[u], "src", source_count, u).astype(F32))
        summed = functools.reduce(jnp.add, moved)
        summed = summed.reshape((half, 2) + summed.shape[1:])
        for t in list(range(base, base + half))[::-1]:
            value = summed[t - base]
            kept.append(sends(value.astype(BF16), t).astype(F32) if t else value)
    return functools.reduce(jnp.add, kept[::-1])[None]


def solution(mesh):
    placed = (
        P("src", "snk", None, None, None),
        P("snk", None, None, "src", None),
        P("snk"),
        P("src", None, None, None),
        P("src", None, None),
        P(),
    )
    return jax.shard_map(
        on_device,
        mesh=mesh,
        in_specs=placed,
        out_specs=P("snk", None, "src", None),
        check_vma=False,
    )
```

time: 429 us -> 163 us (0.38)
  waiting for transfers between devices: 281 us -> 59.2 us
  matrix products: 75 us -> 0 us
  local copies, waits for them, and re-layouts: 50.7 us -> 3.05 us
  Pallas kernels: 0 us -> 41.8 us
  starting transfers between devices: 5.15 us -> 36.7 us
  blocking collectives: 0 us -> 19.1 us
  between operations: 14 us -> 0.98 us
    all_to_all x1 -> x0, waiting for transfers between devices: 176 us -> none  [on_device(): lax.all_to_all(packed, 'snk', split_axis=0, concat_axis=0, tiled=True)]
    dot_general x11 -> x0, matrix products: 75 us -> none  [the longest x1 29.9 us: on_device(): jnp.einsum('nkc,kcxrm->nxrm', weights, products, precision=lax.Precision....]
    ppermute x0 -> x24, waiting for transfers between devices: none -> 59.2 us  [swap(): return lax.ppermute(value, axis, [(i, i ^ flip) for i in range(size)])]
    unnamed x4 -> x0, waiting for transfers between devices: 51.4 us -> none
    pallas_call x0 -> x8, Pallas kernels: none -> 41.8 us  [the longest x3 23.1 us: dress(): pl.pallas_call(functools.partial(dress_kernel, spin, pieces), out_shape=o...]
    ppermute x0 -> x24, starting transfers between devices: none -> 36.7 us  [swap(): return lax.ppermute(value, axis, [(i, i ^ flip) for i in range(size)])]
    reduce_scatter x1 -> x0, waiting for transfers between devices: 32.8 us -> none  [on_device(): return lax.psum_scatter(summed_rows, 'snk', scatter_dimension=0, tiled=True)]
    all_gather x1 -> x0, waiting for transfers between devices: 20.5 us -> none  [on_device(): lax.all_gather(elementals[0], 'src', axis=2, tiled=True)]
  transfers between devices with their start and end apart: 4 -> 24, of which waited for: 4 -> 4; matrix products, arithmetic and copies ran while one was open for 4% -> 1% of each run, Pallas kernels for 0% -> 22%
where the time goes in v1:
time: 163 us; the launch traced here: 162 us
  waiting for transfers between devices  59.2 us (36%)
  Pallas kernels  41.8 us (26%)
  starting transfers between devices  36.7 us (23%)
  blocking collectives  19.1 us (12%)
  local copies, waits for them, and re-layouts  3.05 us (2%)
    ppermute x24, waiting for transfers between devices, swap(): return lax.ppermute(value, axis, [(i, i ^ flip) for i in range(size)])  59.2 us
    ppermute x24, starting transfers between devices, swap(): return lax.ppermute(value, axis, [(i, i ^ flip) for i in range(size)])  36.7 us
    pallas_call x3, Pallas kernels, dress(): pl.pallas_call(functools.partial(dress_kernel, spin, pieces), out_shape=o...  23.1 us
    pallas_call x3, Pallas kernels, finish(): pl.pallas_call(functools.partial(finish_kernel, count, late, nodes, base,...  14.2 us
    all_gather x1, blocking collectives, on_device(): phi = near_phi = lax.all_gather(piece, 'src', axis=1, tiled=True)  9.7 us
    all_gather x1, blocking collectives, on_device(): far_phi = lax.all_gather(far_piece, 'src', axis=1, tiled=True)  9.41 us
  transfers between devices with their start and end apart: 24, of which 4 were waited for; matrix products, arithmetic and copies ran while one was open for 1% of the time, Pallas kernels for 22%

profile of v1, /device:TPU:0, one launch (start us, length us, event | category | flops | bytes accessed | tf_op | source)
XLA Modules:
  0.0 162.4 jit_solution(1388269412470914213)
XLA Ops:
  0.0 1.9 %cut.1 = bf16[1024,256]{1,0:T(8,128)(2,1)} custom-call(s32[1]{0:T(128)} %bitcast.11.where_ref, bf16[2,1024,1024]{2,1,0:T(8,128)(2,1)} %bitcast.24), custom_call_target="tpu_custom_call" | custom-call | bytes 1048576 | tf_op jit(solution)/shard_map/cut/pallas_call | solution.py:46
  1.9 4.1 %collective-permute-start.1 = (bf16[1024,256]{1,0:T(8,128)(2,1)}, bf16[1024,256]{1,0:T(8,128)(2,1)}, u32[]{:S(2)}, u32[]{:S(2)}) collective-permute-start(bf16[1024,256]{1,0:T(8,128)(2,1)} %cut.1), channel_id=1, source_target_pairs={{0,4},{1,5},{2,6},{3,7},{4,0},{5,1},{6,2},{7,3},{8,12},{9,13},{10,... | collective-permute-start | bytes 1572872 | tf_op jit(solution)/shard_map/ppermute | solution.py:24
  6.7 9.7 %all_gather.6.phi_ref = bf16[2,256,256]{2,1,0:T(8,128)(2,1)} all-gather(bf16[2,64,256]{2,1,0:T(8,128)(2,1)S(1)} %dynamic-slice_bitcast_fusion), channel_id=1, replica_groups=mesh['src'=4,'snk'=8] {'src'}, dimensions={1}, use_global_device_ids=true | all-gather | bytes 327680 | tf_op jit(solution)/shard_map/all_gather | solution.py:324
  16.4 6.5 %dress.3 = (bf16[1024,256]{1,0:T(8,128)(2,1)}, bf16[1024,256]{1,0:T(8,128)(2,1)}) custom-call(s32[1]{0:T(128)} %bitcast.17.where_ref, bf16[2,256,256]{2,1,0:T(8,128)(2,1)} %all_gather.6.phi_ref, bf16[2,1024,1024]{2,1,0:T(8,128)(2,1)} %bitcast.25), custom_call_target="tpu_custom_call" | custom-call | flops 2147483648 | bytes 2097152 | tf_op jit(solution)/shard_map/dress/pallas_call | solution.py:128
  23.6 11.3 %dress.4 = (bf16[1024,256]{1,0:T(8,128)(2,1)}, bf16[1024,256]{1,0:T(8,128)(2,1)}, bf16[1024,256]{1,0:T(8,128)(2,1)}, bf16[1024,256]{1,0:T(8,128)(2,1)}, bf16[1024,256]{1,0:T(8,128)(2,1)}) custom-call(s32[3]{0:T(128)} %pad_add_fusion.where_ref, bf16[2,256,256]{2,1,0:T(8,128)(2,1)} %all_gather.6.phi_ref, bf16[2,1024,1024]{2,1,0:T(8,128)(2,1)} %bitcast.26), custom_call_target="tpu_custom_call" | custom-call | flops 5368709120 | bytes 5242880 | tf_op jit(solution)/shard_map/dress/pallas_call | solution.py:128
  34.9 1.6 %collective-permute-start.9 = (bf16[1024,256]{1,0:T(8,128)(2,1)}, bf16[1024,256]{1,0:T(8,128)(2,1)S(1)}, u32[]{:S(2)}, u32[]{:S(2)}) collective-permute-start(bf16[1024,256]{1,0:T(8,128)(2,1)} %get-tuple-element.36), channel_id=1, source_target_pairs={{0,2},{1,3},{2,0},{3,1},{4,6},{5,7},{6,4},{7,5},{8,10},{9,11},{10,... | collective-permute-start | bytes 1572872 | tf_op jit(solution)/shard_map/ppermute | solution.py:24
  36.8 1.7 %collective-permute-start.7 = (bf16[2,64,256]{2,1,0:T(8,128)(2,1)S(1)}, bf16[2,64,256]{2,1,0:T(8,128)(2,1)S(1)}, u32[]{:S(2)}, u32[]{:S(2)}) collective-permute-start(bf16[2,64,256]{2,1,0:T(8,128)(2,1)S(1)} %dynamic-slice_bitcast_fusion), channel_id=1, source_target_pairs={{0,4},{1,5},{2,6},{3,7},{4,0},{5,1},{6,2},{7,3},{8,12},{9,13},{10,... | collective-permute-start | bytes 196616 | tf_op jit(solution)/shard_map/ppermute | solution.py:24
  38.4 24.0 %collective-permute-done.7 = bf16[2,64,256]{2,1,0:T(8,128)(2,1)S(1)} collective-permute-done((bf16[2,64,256]{2,1,0:T(8,128)(2,1)S(1)}, bf16[2,64,256]{2,1,0:T(8,128)(2,1)S(1)}, u32[]{:S(2)}, u32[]{:S(2)}) %collective-permute-start.7) | collective-permute-done | bytes 65568 | tf_op jit(solution)/shard_map/ppermute | solution.py:24
  62.4 9.4 %all_gather.7.phi_ref = bf16[2,256,256]{2,1,0:T(8,128)(2,1)} all-gather(bf16[2,64,256]{2,1,0:T(8,128)(2,1)S(1)} %collective-permute-done.7), channel_id=1, replica_groups=mesh['src'=4,'snk'=8] {'src'}, dimensions={1}, use_global_device_ids=true | all-gather | bytes 327680 | tf_op jit(solution)/shard_map/all_gather | solution.py:343
  71.9 5.3 %dress.5.refs_2_ = bf16[1024,256]{1,0:T(8,128)(2,1)} custom-call(s32[1]{0:T(128)} %constant.84.clone.1.where_ref, bf16[2,256,256]{2,1,0:T(8,128)(2,1)} %all_gather.7.phi_ref, bf16[1024,256]{1,0:T(8,128)(2,1)} %collective-permute-done.1.tile_ref), custom_call_target="tpu_custom_call" | custom-call | flops 1073741824 | bytes 1048576 | tf_op jit(solution)/shard_map/dress/pallas_call | solution.py:128
  77.8 1.5 collective-permute-start.2
  80.2 2.8 %collective-permute-start.13 = (bf16[1024,256]{1,0:T(8,128)(2,1)}, bf16[1024,256]{1,0:T(8,128)(2,1)S(1)}, u32[]{:S(2)}, u32[]{:S(2)}) collective-permute-start(bf16[1024,256]{1,0:T(8,128)(2,1)} %get-tuple-element.42), channel_id=1, source_target_pairs={{0,6},{1,7},{2,4},{3,5},{4,2},{5,3},{6,0},{7,1},{8,14},{9,15},{10,... | collective-permute-start | bytes 1572872 | tf_op jit(solution)/shard_map/ppermute | solution.py:24
  84.0 32.2 %collective-permute-done.2.refs_2_.refs_4_ = bf16[1024,256]{1,0:T(8,128)(2,1)S(1)} collective-permute-done((bf16[1024,256]{1,0:T(8,128)(2,1)}, bf16[1024,256]{1,0:T(8,128)(2,1)S(1)}, u32[]{:S(2)}, u32[]{:S(2)}) %collective-permute-start.2) | collective-permute-done | bytes 524320 | tf_op jit(solution)/shard_map/ppermute | solution.py:24
  118.8 7.3 %finish.3.refs_1_ = f32[8,64,1024]{2,1,0:T(8,128)S(1)} custom-call(s32[8]{0:T(128)S(1)} %stack.35.sinks_ref, s32[8,16]{1,0:T(8,128)S(1)} %fusion.7.dest_ref, s32[1]{0:T(128)} %bitcast.10.here_ref, bf16[1024,256]{1,0:T(8,128)(2,1)S(1)} %copy-done.2, bf16[1024,256]{1,0:T(8,128)(2,1)S(1)} %copy-done.4, bf16[1024,256]{1,0:T(8,128)(2,1)S(1)} %copy-done.5, ...), custom_call_target="tpu_custom_call" | custom-call | flops 4294967296 | bytes 4194304 | tf_op jit(solution)/shard_map/finish/pallas_call | solution.py:275
  126.2 2.6 %gather.1.refs_0_ = f32[32,64,256]{2,1,0:T(8,128)S(1)} custom-call(s32[8]{0:T(128)S(1)} %stack.35.sinks_ref, s32[8,16]{1,0:T(8,128)S(1)} %fusion.7.dest_ref, bf16[1024,256]{1,0:T(8,128)(2,1)S(1)} %copy-done.1, bf16[1024,256]{1,0:T(8,128)(2,1)S(1)} %collective-permute-done.refs_1_.refs_3_, bf16[1024,256]{1,0:T(8,128)(2,1)S(1)} %collective-permute-done.2.refs_2_.refs_4_, ...), custom_call_target="tpu_custom_call" | custom-call | flops 1572864 | bytes 5242880 | tf_op jit(solution)/shard_map/gather/pallas_call | solution.py:180
  128.8 3.5 %finish.5 = (f32[4,16,1024]{2,1,0:T(8,128)S(1)}, bf16[4,16,1024]{2,1,0:T(8,128)(2,1)S(1)}, bf16[4,16,1024]{2,1,0:T(8,128)(2,1)S(1)}, bf16[4,16,1024]{2,1,0:T(8,128)(2,1)S(1)}) custom-call(s32[8]{0:T(128)S(1)} %stack.35.sinks_ref, s32[8,16]{1,0:T(8,128)S(1)} %fusion.7.dest_ref, s32[1]{0:T(128)} %bitcast.10.here_ref, f32[32,64,256]{2,1,0:T(8,128)S(1)} %gather.1.refs_0_, ...), custom_call_target="tpu_custom_call" | custom-call | flops 2147483648 | bytes 4194304 | tf_op jit(solution)/shard_map/finish/pallas_call | solution.py:275
  132.3 1.5 collective-permute-start.19
  135.8 3.4 %finish.4 = (f32[4,16,1024]{2,1,0:T(8,128)S(1)}, bf16[4,16,1024]{2,1,0:T(8,128)(2,1)S(1)}, bf16[4,16,1024]{2,1,0:T(8,128)(2,1)S(1)}, bf16[4,16,1024]{2,1,0:T(8,128)(2,1)S(1)}) custom-call(s32[8]{0:T(128)S(1)} %stack.35.sinks_ref, s32[8,16]{1,0:T(8,128)S(1)} %fusion.7.dest_ref, s32[1]{0:T(128)} %bitcast.10.here_ref, f32[32,64,256]{2,1,0:T(8,128)S(1)} %gather.1.refs_0_, ...), custom_call_target="tpu_custom_call" | custom-call | flops 2147483648 | bytes 4194304 | tf_op jit(solution)/shard_map/finish/pallas_call | solution.py:275
  139.3 1.5 collective-permute-start.15
  142.9 11.5 %collective-permute-start.22 = (bf16[2,16,1024]{2,1,0:T(8,128)(2,1)S(1)}, bf16[2,16,1024]{2,1,0:T(8,128)(2,1)S(1)}, u32[]{:S(2)}, u32[]{:S(2)}) collective-permute-start(bf16[2,16,1024]{2,1,0:T(8,128)(2,1)S(1)} %get-tuple-element.51), channel_id=1, source_target_pairs={{0,4},{1,5},{2,6},{3,7},{4,0},{5,1},{6,2},{7,3},{8,12},{9,13},{10,... | collective-permute-start | bytes 196616 | tf_op jit(solution)/shard_map/ppermute | solution.py:24
  154.4 1.4 collective-permute-start.23
  155.9 2.9 %collective-permute-start.18 = (bf16[2,16,1024]{2,1,0:T(8,128)(2,1)S(1)}, bf16[2,16,1024]{2,1,0:T(8,128)(2,1)S(1)}, u32[]{:S(2)}, u32[]{:S(2)}) collective-permute-start(bf16[2,16,1024]{2,1,0:T(8,128)(2,1)S(1)} %slice.35), channel_id=1, source_target_pairs={{0,2},{1,3},{2,0},{3,1},{4,6},{5,7},{6,4},{7,5},{8,10},{9,11},{10,... | collective-permute-start | bytes 196616 | tf_op jit(solution)/shard_map/ppermute | solution.py:24
  158.8 1.8 %collective-permute-done.23 = bf16[2,16,1024]{2,1,0:T(8,128)(2,1)S(1)} collective-permute-done((bf16[2,16,1024]{2,1,0:T(8,128)(2,1)S(1)}, bf16[2,16,1024]{2,1,0:T(8,128)(2,1)S(1)}, u32[]{:S(2)}, u32[]{:S(2)}) %collective-permute-start.23) | collective-permute-done | bytes 65568 | tf_op jit(solution)/shard_map/ppermute | solution.py:24
  160.6 1.2 collective-permute-done.18
  (67 shorter events, 10.8 us)
Async XLA Ops:
  1.9 70.0 %collective-permute-start.1 = (bf16[1024,256]{1,0:T(8,128)(2,1)}, bf16[1024,256]{1,0:T(8,128)(2,1)}, u32[]{:S(2)}, u32[]{:S(2)}) collective-permute-start(bf16[1024,256]{1,0:T(8,128)(2,1)} %cut.1), channel_id=1, source_target_pairs={{0,4},{1,5},{2,6},{3,7},{4,0},{5,1},{6,2},{7,3},{8,12},{9,13},{10,... | collective-permute-start | bytes 1572872 | tf_op jit(solution)/shard_map/ppermute | solution.py:24
  34.9 42.4 %collective-permute-start.9 = (bf16[1024,256]{1,0:T(8,128)(2,1)}, bf16[1024,256]{1,0:T(8,128)(2,1)S(1)}, u32[]{:S(2)}, u32[]{:S(2)}) collective-permute-start(bf16[1024,256]{1,0:T(8,128)(2,1)} %get-tuple-element.36), channel_id=1, source_target_pairs={{0,2},{1,3},{2,0},{3,1},{4,6},{5,7},{6,4},{7,5},{8,10},{9,11},{10,... | collective-permute-start | bytes 1572872 | tf_op jit(solution)/shard_map/ppermute | solution.py:24
  36.5 41.3 %collective-permute-start.11 = (bf16[1024,256]{1,0:T(8,128)(2,1)S(1)}, bf16[1024,256]{1,0:T(8,128)(2,1)}, u32[]{:S(2)}, u32[]{:S(2)}) collective-permute-start(bf16[1024,256]{1,0:T(8,128)(2,1)S(1)} %copy-done.10), channel_id=1, source_target_pairs={{0,6},{1,7},{2,4},{3,5},{4,2},{5,3},{6,0},{7,1},{8,14},{9,15},{10,... | collective-permute-start | bytes 1572872 | tf_op jit(solution)/shard_map/ppermute | solution.py:24
  36.8 42.6 %collective-permute-start.6 = (bf16[1024,256]{1,0:T(8,128)(2,1)}, bf16[1024,256]{1,0:T(8,128)(2,1)S(1)}, u32[]{:S(2)}, u32[]{:S(2)}) collective-permute-start(bf16[1024,256]{1,0:T(8,128)(2,1)} %get-tuple-element.38.refs_0_), channel_id=1, source_target_pairs={{0,1},{1,0},{2,3},{3,2},{4,5},{5,4},{6,7},{7,6},{8,9},{9,8},{10,11... | collective-permute-start | bytes 1572872 | tf_op jit(solution)/shard_map/ppermute | solution.py:24
  36.8 25.7 %collective-permute-start.7 = (bf16[2,64,256]{2,1,0:T(8,128)(2,1)S(1)}, bf16[2,64,256]{2,1,0:T(8,128)(2,1)S(1)}, u32[]{:S(2)}, u32[]{:S(2)}) collective-permute-start(bf16[2,64,256]{2,1,0:T(8,128)(2,1)S(1)} %dynamic-slice_bitcast_fusion), channel_id=1, source_target_pairs={{0,4},{1,5},{2,6},{3,7},{4,0},{5,1},{6,2},{7,3},{8,12},{9,13},{10,... | collective-permute-start | bytes 196616 | tf_op jit(solution)/shard_map/ppermute | solution.py:24
  62.4 20.7 %collective-permute-start.4 = (bf16[1024,256]{1,0:T(8,128)(2,1)}, bf16[1024,256]{1,0:T(8,128)(2,1)S(1)}, u32[]{:S(2)}, u32[]{:S(2)}) collective-permute-start(bf16[1024,256]{1,0:T(8,128)(2,1)} %get-tuple-element.37), channel_id=1, source_target_pairs={{0,2},{1,3},{2,0},{3,1},{4,6},{5,7},{6,4},{7,5},{8,10},{9,11},{10,... | collective-permute-start | bytes 1572872 | tf_op jit(solution)/shard_map/ppermute | solution.py:24
  77.2 6.7 %collective-permute-start.8 = (bf16[1024,256]{1,0:T(8,128)(2,1)}, bf16[1024,256]{1,0:T(8,128)(2,1)}, u32[]{:S(2)}, u32[]{:S(2)}) collective-permute-start(bf16[1024,256]{1,0:T(8,128)(2,1)} %dress.5.refs_2_), channel_id=1, source_target_pairs={{0,1},{1,0},{2,3},{3,2},{4,5},{5,4},{6,7},{7,6},{8,9},{9,8},{10,11... | collective-permute-start | bytes 1572872 | tf_op jit(solution)/shard_map/ppermute | solution.py:24
  77.3 6.0 %collective-permute-start.10 = (bf16[1024,256]{1,0:T(8,128)(2,1)S(1)}, bf16[1024,256]{1,0:T(8,128)(2,1)}, u32[]{:S(2)}, u32[]{:S(2)}) collective-permute-start(bf16[1024,256]{1,0:T(8,128)(2,1)S(1)} %collective-permute-done.9.refs_4_), channel_id=1, source_target_pairs={{0,1},{1,0},{2,3},{3,2},{4,5},{5,4},{6,7},{7,6},{8,9},{9,8},{10,11... | collective-permute-start | bytes 1572872 | tf_op jit(solution)/shard_map/ppermute | solution.py:24
  77.8 38.4 %collective-permute-start.2 = (bf16[1024,256]{1,0:T(8,128)(2,1)}, bf16[1024,256]{1,0:T(8,128)(2,1)S(1)}, u32[]{:S(2)}, u32[]{:S(2)}) collective-permute-start(bf16[1024,256]{1,0:T(8,128)(2,1)} %get-tuple-element.34), channel_id=1, source_target_pairs={{0,4},{1,5},{2,6},{3,7},{4,0},{5,1},{6,2},{7,3},{8,12},{9,13},{10,... | collective-permute-start | bytes 1572872 | tf_op jit(solution)/shard_map/ppermute | solution.py:24
  80.2 36.0 %collective-permute-start.13 = (bf16[1024,256]{1,0:T(8,128)(2,1)}, bf16[1024,256]{1,0:T(8,128)(2,1)S(1)}, u32[]{:S(2)}, u32[]{:S(2)}) collective-permute-start(bf16[1024,256]{1,0:T(8,128)(2,1)} %get-tuple-element.42), channel_id=1, source_target_pairs={{0,6},{1,7},{2,4},{3,5},{4,2},{5,3},{6,0},{7,1},{8,14},{9,15},{10,... | collective-permute-start | bytes 1572872 | tf_op jit(solution)/shard_map/ppermute | solution.py:24
  83.1 33.6 %collective-permute-start.12 = (bf16[1024,256]{1,0:T(8,128)(2,1)}, bf16[1024,256]{1,0:T(8,128)(2,1)S(1)}, u32[]{:S(2)}, u32[]{:S(2)}) collective-permute-start(bf16[1024,256]{1,0:T(8,128)(2,1)} %collective-permute-done.11.refs_6_), channel_id=1, source_target_pairs={{0,1},{1,0},{2,3},{3,2},{4,5},{5,4},{6,7},{7,6},{8,9},{9,8},{10,11... | collective-permute-start | bytes 1572872 | tf_op jit(solution)/shard_map/ppermute | solution.py:24
  83.4 42.8 %collective-permute-start = (bf16[1024,256]{1,0:T(8,128)(2,1)S(1)}, bf16[1024,256]{1,0:T(8,128)(2,1)S(1)}, u32[]{:S(2)}, u32[]{:S(2)}) collective-permute-start(bf16[1024,256]{1,0:T(8,128)(2,1)S(1)} %copy-done.1), channel_id=1, source_target_pairs={{0,1},{1,0},{2,3},{3,2},{4,5},{5,4},{6,7},{7,6},{8,9},{9,8},{10,11... | collective-permute-start | bytes 1572872 | tf_op jit(solution)/shard_map/ppermute | solution.py:24
  83.9 42.3 %collective-permute-start.5 = (bf16[1024,256]{1,0:T(8,128)(2,1)S(1)}, bf16[1024,256]{1,0:T(8,128)(2,1)S(1)}, u32[]{:S(2)}, u32[]{:S(2)}) collective-permute-start(bf16[1024,256]{1,0:T(8,128)(2,1)S(1)} %collective-permute-done.4.refs_4_.refs_6_), channel_id=1, source_target_pairs={{0,1},{1,0},{2,3},{3,2},{4,5},{5,4},{6,7},{7,6},{8,9},{9,8},{10,11... | collective-permute-start | bytes 1572872 | tf_op jit(solution)/shard_map/ppermute | solution.py:24
  116.2 10.0 %collective-permute-start.3 = (bf16[1024,256]{1,0:T(8,128)(2,1)S(1)}, bf16[1024,256]{1,0:T(8,128)(2,1)S(1)}, u32[]{:S(2)}, u32[]{:S(2)}) collective-permute-start(bf16[1024,256]{1,0:T(8,128)(2,1)S(1)} %collective-permute-done.2.refs_2_.refs_4_), channel_id=1, source_target_pairs={{0,1},{1,0},{2,3},{3,2},{4,5},{5,4},{6,7},{7,6},{8,9},{9,8},{10,11... | collective-permute-start | bytes 1572872 | tf_op jit(solution)/shard_map/ppermute | solution.py:24
  116.2 12.6 %collective-permute-start.14 = (bf16[1024,256]{1,0:T(8,128)(2,1)S(1)}, bf16[1024,256]{1,0:T(8,128)(2,1)S(1)}, u32[]{:S(2)}, u32[]{:S(2)}) collective-permute-start(bf16[1024,256]{1,0:T(8,128)(2,1)S(1)} %collective-permute-done.13.refs_8_), channel_id=1, source_target_pairs={{0,1},{1,0},{2,3},{3,2},{4,5},{5,4},{6,7},{7,6},{8,9},{9,8},{10,11... | collective-permute-start | bytes 1572872 | tf_op jit(solution)/shard_map/ppermute | solution.py:24
  132.3 9.5 %collective-permute-start.19 = (bf16[4,16,1024]{2,1,0:T(8,128)(2,1)S(1)}, bf16[4,16,1024]{2,1,0:T(8,128)(2,1)S(1)}, u32[]{:S(2)}, u32[]{:S(2)}) collective-permute-start(bf16[4,16,1024]{2,1,0:T(8,128)(2,1)S(1)} %get-tuple-element.48), channel_id=1, source_target_pairs={{0,24},{8,16},{16,8},{24,0},{1,25},{9,17},{17,9},{25,1},{2,26},{10... | collective-permute-start | bytes 393224 | tf_op jit(solution)/shard_map/ppermute | solution.py:24
  133.8 9.0 %collective-permute-start.20 = (bf16[4,16,1024]{2,1,0:T(8,128)(2,1)S(1)}, bf16[4,16,1024]{2,1,0:T(8,128)(2,1)S(1)}, u32[]{:S(2)}, u32[]{:S(2)}) collective-permute-start(bf16[4,16,1024]{2,1,0:T(8,128)(2,1)S(1)} %get-tuple-element.49), channel_id=1, source_target_pairs={{0,16},{8,24},{16,0},{24,8},{1,17},{9,25},{17,1},{25,9},{2,18},{10... | collective-permute-start | bytes 393224 | tf_op jit(solution)/shard_map/ppermute | solution.py:24
  134.7 8.1 %collective-permute-start.21 = (bf16[4,16,1024]{2,1,0:T(8,128)(2,1)S(1)}, bf16[4,16,1024]{2,1,0:T(8,128)(2,1)S(1)}, u32[]{:S(2)}, u32[]{:S(2)}) collective-permute-start(bf16[4,16,1024]{2,1,0:T(8,128)(2,1)S(1)} %get-tuple-element.50), channel_id=1, source_target_pairs={{0,8},{8,0},{16,24},{24,16},{1,9},{9,1},{17,25},{25,17},{2,10},{10... | collective-permute-start | bytes 393224 | tf_op jit(solution)/shard_map/ppermute | solution.py:24
  139.3 16.5 %collective-permute-start.15 = (bf16[4,16,1024]{2,1,0:T(8,128)(2,1)S(1)}, bf16[4,16,1024]{2,1,0:T(8,128)(2,1)S(1)}, u32[]{:S(2)}, u32[]{:S(2)}) collective-permute-start(bf16[4,16,1024]{2,1,0:T(8,128)(2,1)S(1)} %get-tuple-element.44), channel_id=1, source_target_pairs={{0,24},{8,16},{16,8},{24,0},{1,25},{9,17},{17,9},{25,1},{2,26},{10... | collective-permute-start | bytes 393224 | tf_op jit(solution)/shard_map/ppermute | solution.py:24
  140.8 15.0 %collective-permute-start.16 = (bf16[4,16,1024]{2,1,0:T(8,128)(2,1)S(1)}, bf16[4,16,1024]{2,1,0:T(8,128)(2,1)S(1)}, u32[]{:S(2)}, u32[]{:S(2)}) collective-permute-start(bf16[4,16,1024]{2,1,0:T(8,128)(2,1)S(1)} %get-tuple-element.45), channel_id=1, source_target_pairs={{0,16},{8,24},{16,0},{24,8},{1,17},{9,25},{17,1},{25,9},{2,18},{10... | collective-permute-start | bytes 393224 | tf_op jit(solution)/shard_map/ppermute | solution.py:24
  141.7 14.0 %collective-permute-start.17 = (bf16[4,16,1024]{2,1,0:T(8,128)(2,1)S(1)}, bf16[4,16,1024]{2,1,0:T(8,128)(2,1)S(1)}, u32[]{:S(2)}, u32[]{:S(2)}) collective-permute-start(bf16[4,16,1024]{2,1,0:T(8,128)(2,1)S(1)} %get-tuple-element.46), channel_id=1, source_target_pairs={{0,8},{8,0},{16,24},{24,16},{1,9},{9,1},{17,25},{25,17},{2,10},{10... | collective-permute-start | bytes 393224 | tf_op jit(solution)/shard_map/ppermute | solution.py:24
  142.9 15.8 %collective-permute-start.22 = (bf16[2,16,1024]{2,1,0:T(8,128)(2,1)S(1)}, bf16[2,16,1024]{2,1,0:T(8,128)(2,1)S(1)}, u32[]{:S(2)}, u32[]{:S(2)}) collective-permute-start(bf16[2,16,1024]{2,1,0:T(8,128)(2,1)S(1)} %get-tuple-element.51), channel_id=1, source_target_pairs={{0,4},{1,5},{2,6},{3,7},{4,0},{5,1},{6,2},{7,3},{8,12},{9,13},{10,... | collective-permute-start | bytes 196616 | tf_op jit(solution)/shard_map/ppermute | solution.py:24
  154.4 6.2 %collective-permute-start.23 = (bf16[2,16,1024]{2,1,0:T(8,128)(2,1)S(1)}, bf16[2,16,1024]{2,1,0:T(8,128)(2,1)S(1)}, u32[]{:S(2)}, u32[]{:S(2)}) collective-permute-start(bf16[2,16,1024]{2,1,0:T(8,128)(2,1)S(1)} %get-tuple-element.52), channel_id=1, source_target_pairs={{0,6},{1,7},{2,4},{3,5},{4,2},{5,3},{6,0},{7,1},{8,14},{9,15},{10,... | collective-permute-start | bytes 196616 | tf_op jit(solution)/shard_map/ppermute | solution.py:24
  155.9 5.9 %collective-permute-start.18 = (bf16[2,16,1024]{2,1,0:T(8,128)(2,1)S(1)}, bf16[2,16,1024]{2,1,0:T(8,128)(2,1)S(1)}, u32[]{:S(2)}, u32[]{:S(2)}) collective-permute-start(bf16[2,16,1024]{2,1,0:T(8,128)(2,1)S(1)} %slice.35), channel_id=1, source_target_pairs={{0,2},{1,3},{2,0},{3,1},{4,6},{5,7},{6,4},{7,5},{8,10},{9,11},{10,... | collective-permute-start | bytes 196616 | tf_op jit(solution)/shard_map/ppermute | solution.py:24
  (11 other events, 124.5 us)

commit v2 on v1

--- a/solution.py
+++ b/solution.py
@@ -24,31 +24,48 @@
     return lax.ppermute(value, axis, [(i, i ^ flip) for i in range(size)])
 
 
-def cut_kernel(where_ref, tile_hbm, out_ref, sems):
-    width = out_ref.shape[-1] // 2
-    start = pl.multiple_of(where_ref[0] * width, width)
-    copies = [
-        pltpu.make_async_copy(
-            tile_hbm.at[x, :, pl.ds(start, width)],
-            out_ref.at[:, x * width : (x + 1) * width],
-            sems.at[x],
-        )
-        for x in range(2)
-    ]
-    for copy in copies:
+def cut_kernel(steps, where_ref, tile_hbm, out_hbm, held_ref, in_sems, out_sems):
+    order, width = held_ref.shape
+    half = width // 2
+    start = pl.multiple_of(where_ref[0] * half, half)
+    rows = order // steps
+    into, out = [], []
+    for i in range(steps):
+        span = slice(i * rows, (i + 1) * rows)
+        for x in range(2):
+            held = held_ref.at[span, x * half : (x + 1) * half]
+            into.append(
+                pltpu.make_async_copy(
+                    tile_hbm.at[x, span, pl.ds(start, half)], held, in_sems.at[2 * i + x]
+                )
+            )
+            out.append(
+                pltpu.make_async_copy(
+                    held, out_hbm.at[span, x * half : (x + 1) * half], out_sems.at[2 * i + x]
+                )
+            )
+    for copy in into:
         copy.start()
-    for copy in copies:
+    for copy, onward in zip(into, out):
         copy.wait()
+        onward.start()
+    for onward in out:
+        onward.wait()
 
 
 def cut(tile, where, width):
     _, order, _ = tile.shape
+    steps = 4
     return pl.pallas_call(
-        cut_kernel,
+        functools.partial(cut_kernel, steps),
         out_shape=jax.ShapeDtypeStruct((order, 2 * width), tile.dtype),
         in_specs=[SMEM, ANY],
-        out_specs=VMEM,
-        scratch_shapes=[pltpu.SemaphoreType.DMA((2,))],
+        out_specs=ANY,
+        scratch_shapes=[
+            pltpu.VMEM((order, 2 * width), tile.dtype),
+            pltpu.SemaphoreType.DMA((2 * steps,)),
+            pltpu.SemaphoreType.DMA((2 * steps,)),
+        ],
         compiler_params=params(60),
         cost_estimate=pl.CostEstimate(
             flops=0, bytes_accessed=8 * order * width, transcendentals=0
@@ -215,7 +232,7 @@
             sums_ref[i] = early_ref[start + i]
             return carry
 
-        lax.fori_loop(0, groups, take, 0)
+        lax.fori_loop(0, groups, take, 0, unroll=4)
     for i in range(count - late, count):
         add_slabs(dest_ref, sinks_ref[i], tiles[i], sums_ref, start)
 
@@ -232,7 +249,7 @@
             left_ref[pl.ds(rows + slab_rows, slab_rows), two] = -real
         return carry
 
-    lax.fori_loop(0, nodes, place, 0)
+    lax.fori_loop(0, nodes, place, 0, unroll=True)
     block = 256
 
     def multiply(j, carry):
@@ -249,7 +266,7 @@
         total_ref[:, :, cols] = product.reshape(2 * nodes, slab_rows, block)
         return carry
 
-    lax.fori_loop(0, order // block, multiply, 0)
+    lax.fori_loop(0, order // block, multiply, 0, unroll=True)
     if last:
         rows = slab_rows // len(outs)
         for u, out_ref in enumerate(outs):
@@ -317,30 +334,29 @@
     part = width // chunks
     tie = lax.optimization_barrier
 
+    piece = lax.dynamic_index_in_dim(elementals[0], momentum[0], 0, False)
+    far_piece = sends(piece, raw)
     first = cut(tile, column(raw) * chunks, part)
     far_raw = sends(first, raw)
-    piece = lax.dynamic_index_in_dim(elementals[0], momentum[0], 0, False)
-    piece, first = tie((piece, first))
-    phi = near_phi = lax.all_gather(piece, "src", axis=1, tiled=True)
+    phi = lax.all_gather(piece, "src", axis=1, tiled=True)
+    far_phi = lax.all_gather(far_piece, "src", axis=1, tiled=True)
     own = {}
-    (own[steps[-1]],) = dress(phi, spin, tile, column(steps[-1]), [width], [chunks])
-    phi, own[steps[-1]] = tie((phi, own[steps[-1]]))
-    rest = ([raw] if chunks > 1 else []) + steps[-2::-1] + [0]
-    where = [column(t) * chunks + 1 if t == raw else column(t) for t in rest]
+    next_t = steps[-1]
+    (next_first,) = dress(phi, spin, tile, column(next_t) * chunks, [part], [1])[0]
+    phi, next_first = tie((phi, next_first))
+    rest = [(raw, 1), (next_t, 1)] if chunks > 1 else []
+    rest += [(t, 0) for t in steps[-2::-1] + [0]]
     made = dress(
         phi,
         spin,
         tile,
-        jnp.concatenate(where),
-        [part if t == raw else width for t in rest],
-        [1 if t == raw else chunks for t in rest],
+        jnp.concatenate([column(t) * chunks + 1 if c else column(t) for t, c in rest]),
+        [part if c else width for t, c in rest],
+        [1 if c else chunks for t, c in rest],
     )
-    own.update(zip(rest, made))
-    if chunks > 1:
-        own[raw] = [None] + own[raw]
-    piece, near_phi = tie((piece, near_phi))
-    far_piece = sends(piece, raw)
-    far_phi = lax.all_gather(far_piece, "src", axis=1, tiled=True)
+    for (t, c), arrays in zip(rest, made):
+        own[t] = [None] * c + list(arrays)
+    own.setdefault(next_t, [None])[0] = next_first
 
     here = source.astype(jnp.int32).reshape(1)
     arrival = [0, raw] + steps

time: 163 us -> 149 us (0.914)
  waiting for transfers between devices: 59.2 us -> 50.1 us
  starting transfers between devices: 36.7 us -> 33.8 us
  Pallas kernels: 41.8 us -> 39.5 us
    ppermute x24, waiting for transfers between devices: 59.2 us -> 50.1 us  [swap(): return lax.ppermute(value, axis, [(i, i ^ flip) for i in range(size)])]
    pallas_call x3, Pallas kernels: 14.2 us -> 11.3 us  [finish(): pl.pallas_call(functools.partial(finish_kernel, count, late, nodes, base,...]
    ppermute x24, starting transfers between devices: 36.7 us -> 33.8 us  [swap(): return lax.ppermute(value, axis, [(i, i ^ flip) for i in range(size)])]
  transfers between devices with their start and end apart: 24 -> 24, of which waited for: 4 -> 6; matrix products, arithmetic and copies ran while one was open for 1% -> 1% of each run, Pallas kernels for 22% -> 21%
where the time goes in v2:
time: 149 us; the launch traced here: 148 us
  waiting for transfers between devices  50.1 us (34%)
  Pallas kernels  39.5 us (27%)
  starting transfers between devices  33.8 us (23%)
  blocking collectives  20.7 us (14%)
  other arithmetic  1.61 us (1%)
    ppermute x24, waiting for transfers between devices, swap(): return lax.ppermute(value, axis, [(i, i ^ flip) for i in range(size)])  50.1 us
    ppermute x24, starting transfers between devices, swap(): return lax.ppermute(value, axis, [(i, i ^ flip) for i in range(size)])  33.8 us
    pallas_call x3, Pallas kernels, dress(): pl.pallas_call(functools.partial(dress_kernel, spin, pieces), out_shape=o...  23.7 us
    pallas_call x3, Pallas kernels, finish(): pl.pallas_call(functools.partial(finish_kernel, count, late, nodes, base,...  11.3 us
    all_gather x1, blocking collectives, on_device(): phi = lax.all_gather(piece, 'src', axis=1, tiled=True)  11.2 us
    all_gather x1, blocking collectives, on_device(): far_phi = lax.all_gather(far_piece, 'src', axis=1, tiled=True)  9.55 us
  transfers between devices with their start and end apart: 24, of which 6 were waited for; matrix products, arithmetic and copies ran while one was open for 1% of the time, Pallas kernels for 21%

profile of v2, /device:TPU:0, one launch (start us, length us, event | category | flops | bytes accessed | tf_op | source)
XLA Modules:
  0.0 148.2 jit_solution(10686647572407008365)
XLA Ops:
  1.0 11.2 %all-gather = bf16[1,1,2,256,256]{4,3,2,1,0:T(8,128)(2,1)} all-gather(bf16[1,1,2,64,256]{4,3,2,1,0:T(8,128)(2,1)S(1)} %constant_dynamic-slice_fusion), channel_id=2, replica_groups=mesh['src'=4,'snk'=8] {'src'}, dimensions={3}, use_global_device_ids=true | all-gather | bytes 327680 | tf_op jit(solution)/shard_map/all_gather | solution.py:341
  12.1 5.2 %dress.3 = bf16[1024,256]{1,0:T(8,128)(2,1)} custom-call(s32[1]{0:T(128)} %bitcast.12.where_ref, bf16[2,256,256]{2,1,0:T(8,128)(2,1)} %bitcast.28, bf16[2,1024,1024]{2,1,0:T(8,128)(2,1)} %bitcast.25), custom_call_target="tpu_custom_call" | custom-call | flops 1073741824 | bytes 1048576 | tf_op jit(solution)/shard_map/dress/pallas_call | solution.py:145
  17.4 3.7 %collective-permute-start.11 = (bf16[1024,256]{1,0:T(8,128)(2,1)}, bf16[1024,256]{1,0:T(8,128)(2,1)S(1)}, u32[]{:S(2)}, u32[]{:S(2)}) collective-permute-start(bf16[1024,256]{1,0:T(8,128)(2,1)} %dress.3), channel_id=1, source_target_pairs={{0,6},{1,7},{2,4},{3,5},{4,2},{5,3},{6,0},{7,1},{8,14},{9,15},{10,... | collective-permute-start | bytes 1572872 | tf_op jit(solution)/shard_map/ppermute | solution.py:24
  21.1 1.9 %cut.1 = bf16[1024,256]{1,0:T(8,128)(2,1)} custom-call(s32[1]{0:T(128)} %bitcast.11.where_ref, bf16[2,1024,1024]{2,1,0:T(8,128)(2,1)} %bitcast.26), custom_call_target="tpu_custom_call" | custom-call | bytes 1048576 | tf_op jit(solution)/shard_map/cut/pallas_call | solution.py:59
  23.7 13.2 %dress.4 = (bf16[1024,256]{1,0:T(8,128)(2,1)}, bf16[1024,256]{1,0:T(8,128)(2,1)}, bf16[1024,256]{1,0:T(8,128)(2,1)}, bf16[1024,256]{1,0:T(8,128)(2,1)}, bf16[102...) custom-call(s32[4]{0:T(128)} %pad_add_fusion.where_ref, bf16[2,256,256]{2,1,0:T(8,128)(2,1)} %bitcast.29, ...), custom_call_target="tpu_custom_call" | custom-call | flops 6442450944 | bytes 6291456 | tf_op jit(solution)/shard_map/dress/pallas_call | solution.py:145
  37.7 1.3 collective-permute-start.4
  39.0 25.4 %collective-permute-done.1.tile_ref = bf16[1024,256]{1,0:T(8,128)(2,1)S(1)} collective-permute-done((bf16[1024,256]{1,0:T(8,128)(2,1)}, bf16[1024,256]{1,0:T(8,128)(2,1)S(1)}, u32[]{:S(2)}, u32[]{:S(2)}) %collective-permute-start.1) | collective-permute-done | bytes 524320 | tf_op jit(solution)/shard_map/ppermute | solution.py:24
  65.0 4.9 %collective-permute-done.7 = bf16[2,64,256]{2,1,0:T(8,128)(2,1)S(1)} collective-permute-done((bf16[2,64,256]{2,1,0:T(8,128)(2,1)S(1)}, bf16[2,64,256]{2,1,0:T(8,128)(2,1)S(1)}, u32[]{:S(2)}, u32[]{:S(2)}) %collective-permute-start.7) | collective-permute-done | bytes 65568 | tf_op jit(solution)/shard_map/ppermute | solution.py:24
  69.9 2.3 %collective-permute-start.13 = (bf16[1024,256]{1,0:T(8,128)(2,1)}, bf16[1024,256]{1,0:T(8,128)(2,1)S(1)}, u32[]{:S(2)}, u32[]{:S(2)}) collective-permute-start(bf16[1024,256]{1,0:T(8,128)(2,1)} %get-tuple-element.34), channel_id=1, source_target_pairs={{0,6},{1,7},{2,4},{3,5},{4,2},{5,3},{6,0},{7,1},{8,14},{9,15},{10,... | collective-permute-start | bytes 1572872 | tf_op jit(solution)/shard_map/ppermute | solution.py:24
  72.4 9.6 %all_gather.7.phi_ref = bf16[2,256,256]{2,1,0:T(8,128)(2,1)} all-gather(bf16[2,64,256]{2,1,0:T(8,128)(2,1)S(1)} %collective-permute-done.7), channel_id=1, replica_groups=mesh['src'=4,'snk'=8] {'src'}, dimensions={1}, use_global_device_ids=true | all-gather | bytes 327680 | tf_op jit(solution)/shard_map/all_gather | solution.py:342
  81.9 5.3 %dress.5.refs_2_ = bf16[1024,256]{1,0:T(8,128)(2,1)} custom-call(s32[1]{0:T(128)} %constant.85.clone.1.where_ref, bf16[2,256,256]{2,1,0:T(8,128)(2,1)} %all_gather.7.phi_ref, bf16[1024,256]{1,0:T(8,128)(2,1)} %copy-done.8), custom_call_target="tpu_custom_call" | custom-call | flops 1073741824 | bytes 1048576 | tf_op jit(solution)/shard_map/dress/pallas_call | solution.py:145
  88.1 16.9 %collective-permute-done.2.refs_2_.refs_4_ = bf16[1024,256]{1,0:T(8,128)(2,1)S(1)} collective-permute-done((bf16[1024,256]{1,0:T(8,128)(2,1)}, bf16[1024,256]{1,0:T(8,128)(2,1)S(1)}, u32[]{:S(2)}, u32[]{:S(2)}) %collective-permute-start.2) | collective-permute-done | bytes 524320 | tf_op jit(solution)/shard_map/ppermute | solution.py:24
  106.6 6.2 %finish.3.refs_1_ = f32[8,64,1024]{2,1,0:T(8,128)S(1)} custom-call(s32[8]{0:T(128)S(1)} %stack.35.sinks_ref, s32[8,16]{1,0:T(8,128)S(1)} %fusion.7.dest_ref, s32[1]{0:T(128)} %bitcast.10.here_ref, bf16[1024,256]{1,0:T(8,128)(2,1)S(1)} %copy-done.2, bf16[1024,256]{1,0:T(8,128)(2,1)S(1)} %collective-permute-done.6.refs_1_, bf16[1024,256]{1,0:T(8,128)(2,1)S(1)} %copy-done.3, ...), custom_call_target="tpu_custom_call" | custom-call | flops 4294967296 | bytes 4194304 | tf_op jit(solution)/shard_map/finish/pallas_call | solution.py:292
  112.8 2.6 %gather.1.refs_0_ = f32[32,64,256]{2,1,0:T(8,128)S(1)} custom-call(s32[8]{0:T(128)S(1)} %stack.35.sinks_ref, s32[8,16]{1,0:T(8,128)S(1)} %fusion.7.dest_ref, bf16[1024,256]{1,0:T(8,128)(2,1)S(1)} %copy-done.1, bf16[1024,256]{1,0:T(8,128)(2,1)S(1)} %collective-permute-done.refs_1_.refs_3_, bf16[1024,256]{1,0:T(8,128)(2,1)S(1)} %collective-permute-done.2.refs_2_.refs_4_, ...), custom_call_target="tpu_custom_call" | custom-call | flops 1572864 | bytes 5242880 | tf_op jit(solution)/shard_map/gather/pallas_call | solution.py:197
  115.4 2.6 %finish.5 = (f32[4,16,1024]{2,1,0:T(8,128)S(1)}, bf16[4,16,1024]{2,1,0:T(8,128)(2,1)S(1)}, bf16[4,16,1024]{2,1,0:T(8,128)(2,1)S(1)}, bf16[4,16,1024]{2,1,0:T(8,128)(2,1)S(1)}) custom-call(s32[8]{0:T(128)S(1)} %stack.35.sinks_ref, s32[8,16]{1,0:T(8,128)S(1)} %fusion.7.dest_ref, s32[1]{0:T(128)} %bitcast.10.here_ref, f32[32,64,256]{2,1,0:T(8,128)S(1)} %gather.1.refs_0_, ...), custom_call_target="tpu_custom_call" | custom-call | flops 2147483648 | bytes 4194304 | tf_op jit(solution)/shard_map/finish/pallas_call | solution.py:292
  118.0 1.5 %collective-permute-start.19 = (bf16[4,16,1024]{2,1,0:T(8,128)(2,1)S(1)}, bf16[4,16,1024]{2,1,0:T(8,128)(2,1)S(1)}, u32[]{:S(2)}, u32[]{:S(2)}) collective-permute-start(bf16[4,16,1024]{2,1,0:T(8,128)(2,1)S(1)} %get-tuple-element.40), channel_id=1, source_target_pairs={{0,24},{8,16},{16,8},{24,0},{1,25},{9,17},{17,9},{25,1},{2,26},{10... | collective-permute-start | bytes 393224 | tf_op jit(solution)/shard_map/ppermute | solution.py:24
  119.5 1.1 collective-permute-start.20
  121.5 2.6 %finish.4 = (f32[4,16,1024]{2,1,0:T(8,128)S(1)}, bf16[4,16,1024]{2,1,0:T(8,128)(2,1)S(1)}, bf16[4,16,1024]{2,1,0:T(8,128)(2,1)S(1)}, bf16[4,16,1024]{2,1,0:T(8,128)(2,1)S(1)}) custom-call(s32[8]{0:T(128)S(1)} %stack.35.sinks_ref, s32[8,16]{1,0:T(8,128)S(1)} %fusion.7.dest_ref, s32[1]{0:T(128)} %bitcast.10.here_ref, f32[32,64,256]{2,1,0:T(8,128)S(1)} %gather.1.refs_0_, ...), custom_call_target="tpu_custom_call" | custom-call | flops 2147483648 | bytes 4194304 | tf_op jit(solution)/shard_map/finish/pallas_call | solution.py:292
  124.1 1.5 %collective-permute-start.15 = (bf16[4,16,1024]{2,1,0:T(8,128)(2,1)S(1)}, bf16[4,16,1024]{2,1,0:T(8,128)(2,1)S(1)}, u32[]{:S(2)}, u32[]{:S(2)}) collective-permute-start(bf16[4,16,1024]{2,1,0:T(8,128)(2,1)S(1)} %get-tuple-element.36), channel_id=1, source_target_pairs={{0,24},{8,16},{16,8},{24,0},{1,25},{9,17},{17,9},{25,1},{2,26},{10... | collective-permute-start | bytes 393224 | tf_op jit(solution)/shard_map/ppermute | solution.py:24
  127.8 12.2 %collective-permute-start.22 = (bf16[2,16,1024]{2,1,0:T(8,128)(2,1)S(1)}, bf16[2,16,1024]{2,1,0:T(8,128)(2,1)S(1)}, u32[]{:S(2)}, u32[]{:S(2)}) collective-permute-start(bf16[2,16,1024]{2,1,0:T(8,128)(2,1)S(1)} %get-tuple-element.43), channel_id=1, source_target_pairs={{0,4},{1,5},{2,6},{3,7},{4,0},{5,1},{6,2},{7,3},{8,12},{9,13},{10,... | collective-permute-start | bytes 196616 | tf_op jit(solution)/shard_map/ppermute | solution.py:24
  139.9 1.9 %collective-permute-start.23 = (bf16[2,16,1024]{2,1,0:T(8,128)(2,1)S(1)}, bf16[2,16,1024]{2,1,0:T(8,128)(2,1)S(1)}, u32[]{:S(2)}, u32[]{:S(2)}) collective-permute-start(bf16[2,16,1024]{2,1,0:T(8,128)(2,1)S(1)} %get-tuple-element.44), channel_id=1, source_target_pairs={{0,6},{1,7},{2,4},{3,5},{4,2},{5,3},{6,0},{7,1},{8,14},{9,15},{10,... | collective-permute-start | bytes 196616 | tf_op jit(solution)/shard_map/ppermute | solution.py:24
  142.0 2.7 %collective-permute-start.18 = (bf16[2,16,1024]{2,1,0:T(8,128)(2,1)S(1)}, bf16[2,16,1024]{2,1,0:T(8,128)(2,1)S(1)}, u32[]{:S(2)}, u32[]{:S(2)}) collective-permute-start(bf16[2,16,1024]{2,1,0:T(8,128)(2,1)S(1)} %slice.35), channel_id=1, source_target_pairs={{0,2},{1,3},{2,0},{3,1},{4,6},{5,7},{6,4},{7,5},{8,10},{9,11},{10,... | collective-permute-start | bytes 196616 | tf_op jit(solution)/shard_map/ppermute | solution.py:24
  145.0 1.2 collective-permute-done.23
  146.2 1.3 collective-permute-done.18
  (64 shorter events, 9.0 us)
Async XLA Ops:
  17.4 47.0 %collective-permute-start.11 = (bf16[1024,256]{1,0:T(8,128)(2,1)}, bf16[1024,256]{1,0:T(8,128)(2,1)S(1)}, u32[]{:S(2)}, u32[]{:S(2)}) collective-permute-start(bf16[1024,256]{1,0:T(8,128)(2,1)} %dress.3), channel_id=1, source_target_pairs={{0,6},{1,7},{2,4},{3,5},{4,2},{5,3},{6,0},{7,1},{8,14},{9,15},{10,... | collective-permute-start | bytes 1572872 | tf_op jit(solution)/shard_map/ppermute | solution.py:24
  22.9 41.5 %collective-permute-start.1 = (bf16[1024,256]{1,0:T(8,128)(2,1)}, bf16[1024,256]{1,0:T(8,128)(2,1)S(1)}, u32[]{:S(2)}, u32[]{:S(2)}) collective-permute-start(bf16[1024,256]{1,0:T(8,128)(2,1)} %cut.1), channel_id=1, source_target_pairs={{0,4},{1,5},{2,6},{3,7},{4,0},{5,1},{6,2},{7,3},{8,12},{9,13},{10,... | collective-permute-start | bytes 1572872 | tf_op jit(solution)/shard_map/ppermute | solution.py:24
  36.9 27.6 %collective-permute-start.9 = (bf16[1024,256]{1,0:T(8,128)(2,1)}, bf16[1024,256]{1,0:T(8,128)(2,1)S(1)}, u32[]{:S(2)}, u32[]{:S(2)}) collective-permute-start(bf16[1024,256]{1,0:T(8,128)(2,1)} %get-tuple-element.29), channel_id=1, source_target_pairs={{0,2},{1,3},{2,0},{3,1},{4,6},{5,7},{6,4},{7,5},{8,10},{9,11},{10,... | collective-permute-start | bytes 1572872 | tf_op jit(solution)/shard_map/ppermute | solution.py:24
  37.7 32.2 %collective-permute-start.6 = (bf16[1024,256]{1,0:T(8,128)(2,1)}, bf16[1024,256]{1,0:T(8,128)(2,1)S(1)}, u32[]{:S(2)}, u32[]{:S(2)}) collective-permute-start(bf16[1024,256]{1,0:T(8,128)(2,1)} %get-tuple-element.31.refs_0_), channel_id=1, source_target_pairs={{0,1},{1,0},{2,3},{3,2},{4,5},{5,4},{6,7},{7,6},{8,9},{9,8},{10,11... | collective-permute-start | bytes 1572872 | tf_op jit(solution)/shard_map/ppermute | solution.py:24
  37.7 49.5 %collective-permute-start.4 = (bf16[1024,256]{1,0:T(8,128)(2,1)}, bf16[1024,256]{1,0:T(8,128)(2,1)S(1)}, u32[]{:S(2)}, u32[]{:S(2)}) collective-permute-start(bf16[1024,256]{1,0:T(8,128)(2,1)} %get-tuple-element.30), channel_id=1, source_target_pairs={{0,2},{1,3},{2,0},{3,1},{4,6},{5,7},{6,4},{7,5},{8,10},{9,11},{10,... | collective-permute-start | bytes 1572872 | tf_op jit(solution)/shard_map/ppermute | solution.py:24
  64.4 5.5 %collective-permute-start.7 = (bf16[2,64,256]{2,1,0:T(8,128)(2,1)S(1)}, bf16[2,64,256]{2,1,0:T(8,128)(2,1)S(1)}, u32[]{:S(2)}, u32[]{:S(2)}) collective-permute-start(bf16[2,64,256]{2,1,0:T(8,128)(2,1)S(1)} %fusion.19), channel_id=1, source_target_pairs={{0,4},{1,5},{2,6},{3,7},{4,0},{5,1},{6,2},{7,3},{8,12},{9,13},{10,... | collective-permute-start | bytes 196616 | tf_op jit(solution)/shard_map/ppermute | solution.py:24
  64.4 23.0 %collective-permute-start.10 = (bf16[1024,256]{1,0:T(8,128)(2,1)S(1)}, bf16[1024,256]{1,0:T(8,128)(2,1)}, u32[]{:S(2)}, u32[]{:S(2)}) collective-permute-start(bf16[1024,256]{1,0:T(8,128)(2,1)S(1)} %collective-permute-done.9.refs_4_), channel_id=1, source_target_pairs={{0,1},{1,0},{2,3},{3,2},{4,5},{5,4},{6,7},{7,6},{8,9},{9,8},{10,11... | collective-permute-start | bytes 1572872 | tf_op jit(solution)/shard_map/ppermute | solution.py:24
  64.5 23.5 %collective-permute-start.12 = (bf16[1024,256]{1,0:T(8,128)(2,1)S(1)}, bf16[1024,256]{1,0:T(8,128)(2,1)}, u32[]{:S(2)}, u32[]{:S(2)}) collective-permute-start(bf16[1024,256]{1,0:T(8,128)(2,1)S(1)} %collective-permute-done.11.refs_6_), channel_id=1, source_target_pairs={{0,1},{1,0},{2,3},{3,2},{4,5},{5,4},{6,7},{7,6},{8,9},{9,8},{10,11... | collective-permute-start | bytes 1572872 | tf_op jit(solution)/shard_map/ppermute | solution.py:24
  69.9 35.1 %collective-permute-start.2 = (bf16[1024,256]{1,0:T(8,128)(2,1)}, bf16[1024,256]{1,0:T(8,128)(2,1)S(1)}, u32[]{:S(2)}, u32[]{:S(2)}) collective-permute-start(bf16[1024,256]{1,0:T(8,128)(2,1)} %get-tuple-element.27), channel_id=1, source_target_pairs={{0,4},{1,5},{2,6},{3,7},{4,0},{5,1},{6,2},{7,3},{8,12},{9,13},{10,... | collective-permute-start | bytes 1572872 | tf_op jit(solution)/shard_map/ppermute | solution.py:24
  69.9 35.0 %collective-permute-start.13 = (bf16[1024,256]{1,0:T(8,128)(2,1)}, bf16[1024,256]{1,0:T(8,128)(2,1)S(1)}, u32[]{:S(2)}, u32[]{:S(2)}) collective-permute-start(bf16[1024,256]{1,0:T(8,128)(2,1)} %get-tuple-element.34), channel_id=1, source_target_pairs={{0,6},{1,7},{2,4},{3,5},{4,2},{5,3},{6,0},{7,1},{8,14},{9,15},{10,... | collective-permute-start | bytes 1572872 | tf_op jit(solution)/shard_map/ppermute | solution.py:24
  87.2 18.3 %collective-permute-start.8 = (bf16[1024,256]{1,0:T(8,128)(2,1)}, bf16[1024,256]{1,0:T(8,128)(2,1)S(1)}, u32[]{:S(2)}, u32[]{:S(2)}) collective-permute-start(bf16[1024,256]{1,0:T(8,128)(2,1)} %dress.5.refs_2_), channel_id=1, source_target_pairs={{0,1},{1,0},{2,3},{3,2},{4,5},{5,4},{6,7},{7,6},{8,9},{9,8},{10,11... | collective-permute-start | bytes 1572872 | tf_op jit(solution)/shard_map/ppermute | solution.py:24
  87.5 25.3 %collective-permute-start = (bf16[1024,256]{1,0:T(8,128)(2,1)S(1)}, bf16[1024,256]{1,0:T(8,128)(2,1)S(1)}, u32[]{:S(2)}, u32[]{:S(2)}) collective-permute-start(bf16[1024,256]{1,0:T(8,128)(2,1)S(1)} %copy-done.1), channel_id=1, source_target_pairs={{0,1},{1,0},{2,3},{3,2},{4,5},{5,4},{6,7},{7,6},{8,9},{9,8},{10,11... | collective-permute-start | bytes 1572872 | tf_op jit(solution)/shard_map/ppermute | solution.py:24
  88.0 24.7 %collective-permute-start.5 = (bf16[1024,256]{1,0:T(8,128)(2,1)S(1)}, bf16[1024,256]{1,0:T(8,128)(2,1)S(1)}, u32[]{:S(2)}, u32[]{:S(2)}) collective-permute-start(bf16[1024,256]{1,0:T(8,128)(2,1)S(1)} %collective-permute-done.4.refs_4_.refs_6_), channel_id=1, source_target_pairs={{0,1},{1,0},{2,3},{3,2},{4,5},{5,4},{6,7},{7,6},{8,9},{9,8},{10,11... | collective-permute-start | bytes 1572872 | tf_op jit(solution)/shard_map/ppermute | solution.py:24
  105.0 7.8 %collective-permute-start.3 = (bf16[1024,256]{1,0:T(8,128)(2,1)S(1)}, bf16[1024,256]{1,0:T(8,128)(2,1)S(1)}, u32[]{:S(2)}, u32[]{:S(2)}) collective-permute-start(bf16[1024,256]{1,0:T(8,128)(2,1)S(1)} %collective-permute-done.2.refs_2_.refs_4_), channel_id=1, source_target_pairs={{0,1},{1,0},{2,3},{3,2},{4,5},{5,4},{6,7},{7,6},{8,9},{9,8},{10,11... | collective-permute-start | bytes 1572872 | tf_op jit(solution)/shard_map/ppermute | solution.py:24
  105.0 10.4 %collective-permute-start.14 = (bf16[1024,256]{1,0:T(8,128)(2,1)S(1)}, bf16[1024,256]{1,0:T(8,128)(2,1)S(1)}, u32[]{:S(2)}, u32[]{:S(2)}) collective-permute-start(bf16[1024,256]{1,0:T(8,128)(2,1)S(1)} %collective-permute-done.13.refs_8_), channel_id=1, source_target_pairs={{0,1},{1,0},{2,3},{3,2},{4,5},{5,4},{6,7},{7,6},{8,9},{9,8},{10,11... | collective-permute-start | bytes 1572872 | tf_op jit(solution)/shard_map/ppermute | solution.py:24
  118.0 8.8 %collective-permute-start.19 = (bf16[4,16,1024]{2,1,0:T(8,128)(2,1)S(1)}, bf16[4,16,1024]{2,1,0:T(8,128)(2,1)S(1)}, u32[]{:S(2)}, u32[]{:S(2)}) collective-permute-start(bf16[4,16,1024]{2,1,0:T(8,128)(2,1)S(1)} %get-tuple-element.40), channel_id=1, source_target_pairs={{0,24},{8,16},{16,8},{24,0},{1,25},{9,17},{17,9},{25,1},{2,26},{10... | collective-permute-start | bytes 393224 | tf_op jit(solution)/shard_map/ppermute | solution.py:24
  119.5 8.2 %collective-permute-start.20 = (bf16[4,16,1024]{2,1,0:T(8,128)(2,1)S(1)}, bf16[4,16,1024]{2,1,0:T(8,128)(2,1)S(1)}, u32[]{:S(2)}, u32[]{:S(2)}) collective-permute-start(bf16[4,16,1024]{2,1,0:T(8,128)(2,1)S(1)} %get-tuple-element.41), channel_id=1, source_target_pairs={{0,16},{8,24},{16,0},{24,8},{1,17},{9,25},{17,1},{25,9},{2,18},{10... | collective-permute-start | bytes 393224 | tf_op jit(solution)/shard_map/ppermute | solution.py:24
  120.6 7.0 %collective-permute-start.21 = (bf16[4,16,1024]{2,1,0:T(8,128)(2,1)S(1)}, bf16[4,16,1024]{2,1,0:T(8,128)(2,1)S(1)}, u32[]{:S(2)}, u32[]{:S(2)}) collective-permute-start(bf16[4,16,1024]{2,1,0:T(8,128)(2,1)S(1)} %get-tuple-element.42), channel_id=1, source_target_pairs={{0,8},{8,0},{16,24},{24,16},{1,9},{9,1},{17,25},{25,17},{2,10},{10... | collective-permute-start | bytes 393224 | tf_op jit(solution)/shard_map/ppermute | solution.py:24
  124.1 17.8 %collective-permute-start.15 = (bf16[4,16,1024]{2,1,0:T(8,128)(2,1)S(1)}, bf16[4,16,1024]{2,1,0:T(8,128)(2,1)S(1)}, u32[]{:S(2)}, u32[]{:S(2)}) collective-permute-start(bf16[4,16,1024]{2,1,0:T(8,128)(2,1)S(1)} %get-tuple-element.36), channel_id=1, source_target_pairs={{0,24},{8,16},{16,8},{24,0},{1,25},{9,17},{17,9},{25,1},{2,26},{10... | collective-permute-start | bytes 393224 | tf_op jit(solution)/shard_map/ppermute | solution.py:24
  125.6 16.2 %collective-permute-start.16 = (bf16[4,16,1024]{2,1,0:T(8,128)(2,1)S(1)}, bf16[4,16,1024]{2,1,0:T(8,128)(2,1)S(1)}, u32[]{:S(2)}, u32[]{:S(2)}) collective-permute-start(bf16[4,16,1024]{2,1,0:T(8,128)(2,1)S(1)} %get-tuple-element.37), channel_id=1, source_target_pairs={{0,16},{8,24},{16,0},{24,8},{1,17},{9,25},{17,1},{25,9},{2,18},{10... | collective-permute-start | bytes 393224 | tf_op jit(solution)/shard_map/ppermute | solution.py:24
  126.8 15.1 %collective-permute-start.17 = (bf16[4,16,1024]{2,1,0:T(8,128)(2,1)S(1)}, bf16[4,16,1024]{2,1,0:T(8,128)(2,1)S(1)}, u32[]{:S(2)}, u32[]{:S(2)}) collective-permute-start(bf16[4,16,1024]{2,1,0:T(8,128)(2,1)S(1)} %get-tuple-element.38), channel_id=1, source_target_pairs={{0,8},{8,0},{16,24},{24,16},{1,9},{9,1},{17,25},{25,17},{2,10},{10... | collective-permute-start | bytes 393224 | tf_op jit(solution)/shard_map/ppermute | solution.py:24
  127.8 17.2 %collective-permute-start.22 = (bf16[2,16,1024]{2,1,0:T(8,128)(2,1)S(1)}, bf16[2,16,1024]{2,1,0:T(8,128)(2,1)S(1)}, u32[]{:S(2)}, u32[]{:S(2)}) collective-permute-start(bf16[2,16,1024]{2,1,0:T(8,128)(2,1)S(1)} %get-tuple-element.43), channel_id=1, source_target_pairs={{0,4},{1,5},{2,6},{3,7},{4,0},{5,1},{6,2},{7,3},{8,12},{9,13},{10,... | collective-permute-start | bytes 196616 | tf_op jit(solution)/shard_map/ppermute | solution.py:24
  139.9 6.2 %collective-permute-start.23 = (bf16[2,16,1024]{2,1,0:T(8,128)(2,1)S(1)}, bf16[2,16,1024]{2,1,0:T(8,128)(2,1)S(1)}, u32[]{:S(2)}, u32[]{:S(2)}) collective-permute-start(bf16[2,16,1024]{2,1,0:T(8,128)(2,1)S(1)} %get-tuple-element.44), channel_id=1, source_target_pairs={{0,6},{1,7},{2,4},{3,5},{4,2},{5,3},{6,0},{7,1},{8,14},{9,15},{10,... | collective-permute-start | bytes 196616 | tf_op jit(solution)/shard_map/ppermute | solution.py:24
  142.0 5.6 %collective-permute-start.18 = (bf16[2,16,1024]{2,1,0:T(8,128)(2,1)S(1)}, bf16[2,16,1024]{2,1,0:T(8,128)(2,1)S(1)}, u32[]{:S(2)}, u32[]{:S(2)}) collective-permute-start(bf16[2,16,1024]{2,1,0:T(8,128)(2,1)S(1)} %slice.35), channel_id=1, source_target_pairs={{0,2},{1,3},{2,0},{3,1},{4,6},{5,7},{6,4},{7,5},{8,10},{9,11},{10,... | collective-permute-start | bytes 196616 | tf_op jit(solution)/shard_map/ppermute | solution.py:24
  (9 other events, 115.8 us)

commit v3 on v2

--- a/solution.py
+++ b/solution.py
@@ -181,23 +181,32 @@
 
         return carry
 
-    lax.fori_loop(0, tile_ref.shape[0] // slab_rows, one, 0)
-
-
-def gather_kernel(count, sinks_ref, dest_ref, *refs):
-    sums_ref = refs[count]
-    clear(sums_ref)
+    lax.fori_loop(0, tile_ref.shape[0] // slab_rows, one, 0, unroll=4)
+
+
+def gather_kernel(count, more, sinks_ref, dest_ref, *refs):
+    sums_ref = refs[-1]
+    if more:
+
+        def take(i, carry):
+            sums_ref[i] = refs[count][i]
+            return carry
+
+        lax.fori_loop(0, sums_ref.shape[0], take, 0, unroll=4)
+    else:
+        clear(sums_ref)
     for i, tile_ref in enumerate(refs[:count]):
         add_slabs(dest_ref, sinks_ref[i], tile_ref, sums_ref)
 
 
-def gather(sinks, dest, tiles, groups):
+def gather(sinks, dest, tiles, groups, before=None):
+    more = [] if before is None else [before]
     order, width = tiles[0].shape
     slab_rows = order // dest.shape[1]
     return pl.pallas_call(
-        functools.partial(gather_kernel, len(tiles)),
+        functools.partial(gather_kernel, len(tiles), bool(more)),
         out_shape=jax.ShapeDtypeStruct((groups, slab_rows, width), F32),
-        in_specs=[SMEM, SMEM] + [VMEM] * len(tiles),
+        in_specs=[SMEM, SMEM] + [VMEM] * (len(tiles) + len(more)),
         out_specs=VMEM,
         compiler_params=params(24),
         cost_estimate=pl.CostEstimate(
@@ -206,7 +215,7 @@
             transcendentals=0,
         ),
         name="gather",
-    )(sinks, dest, *tiles)
+    )(sinks, dest, *tiles, *more)
 
 
 def finish_kernel(count, late, nodes, base, first, last, sinks_ref, dest_ref, here_ref, *refs):
@@ -250,7 +259,7 @@
         return carry
 
     lax.fori_loop(0, nodes, place, 0, unroll=True)
-    block = 256
+    block = 512
 
     def multiply(j, carry):
         cols = pl.ds(pl.multiple_of(j * block, block), block)
@@ -395,8 +404,9 @@
         if c < chunks - 1:
             (total,) = finish(sinks, dest, here, None, total, tiles, count, nodes, 0, 0)
         else:
-            late = 2
-            sums = gather(sinks, dest, tiles[: count - late], sink_count * nodes)
+            late = 1
+            sums = gather(sinks, dest, tiles[: count - 2], sink_count * nodes)
+            sums = gather(sinks[count - 2 :], dest, tiles[-2:-1], sink_count * nodes, sums)
 
     half = nodes // 2
     kept = []
@@ -407,7 +417,7 @@
             moved.append(swap(outs[u], "src", source_count, u).astype(F32))
         summed = functools.reduce(jnp.add, moved)
         summed = summed.reshape((half, 2) + summed.shape[1:])
-        for t in list(range(base, base + half))[::-1]:
+        for t in range(base, base + half):
             value = summed[t - base]
             kept.append(sends(value.astype(BF16), t).astype(F32) if t else value)
     return functools.reduce(jnp.add, kept[::-1])[None]

time: 149 us -> 150 us (level)
  starting transfers between devices: 33.8 us -> 30 us
  waiting for transfers between devices: 50.1 us -> 53.1 us
  Pallas kernels: 39.5 us -> 41.6 us
    ppermute x24, starting transfers between devices: 33.8 us -> 30 us  [swap(): return lax.ppermute(value, axis, [(i, i ^ flip) for i in range(size)])]
    ppermute x24, waiting for transfers between devices: 50.1 us -> 53.1 us  [swap(): return lax.ppermute(value, axis, [(i, i ^ flip) for i in range(size)])]
    pallas_call x1 -> x2, Pallas kernels: 2.56 us -> 3.69 us  [gather(): pl.pallas_call(functools.partial(gather_kernel, len(tiles), bool(more)),...]
  transfers between devices with their start and end apart: 24 -> 24, of which waited for: 6 -> 5; matrix products, arithmetic and copies ran while one was open for 1% -> 1% of each run, Pallas kernels for 21% -> 22%
where the time goes in v3:
time: 150 us; the launch traced here: 149 us
  waiting for transfers between devices  53.1 us (35%)
  Pallas kernels  41.6 us (28%)
  starting transfers between devices  30 us (20%)
  blocking collectives  20.7 us (14%)
  other arithmetic  1.62 us (1%)
    ppermute x24, waiting for transfers between devices, swap(): return lax.ppermute(value, axis, [(i, i ^ flip) for i in range(size)])  53.1 us
    ppermute x24, starting transfers between devices, swap(): return lax.ppermute(value, axis, [(i, i ^ flip) for i in range(size)])  30 us
    pallas_call x3, Pallas kernels, dress(): pl.pallas_call(functools.partial(dress_kernel, spin, pieces), out_shape=o...  23.8 us
    pallas_call x3, Pallas kernels, finish(): pl.pallas_call(functools.partial(finish_kernel, count, late, nodes, base,...  12.2 us
    all_gather x1, blocking collectives, on_device(): phi = lax.all_gather(piece, 'src', axis=1, tiled=True)  11.1 us
    all_gather x1, blocking collectives, on_device(): far_phi = lax.all_gather(far_piece, 'src', axis=1, tiled=True)  9.56 us
    pallas_call x2, Pallas kernels, gather(): pl.pallas_call(functools.partial(gather_kernel, len(tiles), bool(more)),...  3.69 us
  transfers between devices with their start and end apart: 24, of which 5 were waited for; matrix products, arithmetic and copies ran while one was open for 1% of the time, Pallas kernels for 22%

profile of v3, /device:TPU:0, one launch (start us, length us, event | category | flops | bytes accessed | tf_op | source)
XLA Modules:
  0.0 149.2 jit_solution(9599172682240350439)
XLA Ops:
  1.0 11.1 %all-gather = bf16[1,1,2,256,256]{4,3,2,1,0:T(8,128)(2,1)} all-gather(bf16[1,1,2,64,256]{4,3,2,1,0:T(8,128)(2,1)S(1)} %constant_dynamic-slice_fusion), channel_id=2, replica_groups=mesh['src'=4,'snk'=8] {'src'}, dimensions={3}, use_global_device_ids=true | all-gather | bytes 327680 | tf_op jit(solution)/shard_map/all_gather | solution.py:350
  12.1 5.3 %dress.3 = bf16[1024,256]{1,0:T(8,128)(2,1)} custom-call(s32[1]{0:T(128)} %bitcast.12.where_ref, bf16[2,256,256]{2,1,0:T(8,128)(2,1)} %bitcast.28, bf16[2,1024,1024]{2,1,0:T(8,128)(2,1)} %bitcast.25), custom_call_target="tpu_custom_call" | custom-call | flops 1073741824 | bytes 1048576 | tf_op jit(solution)/shard_map/dress/pallas_call | solution.py:145
  17.4 3.7 %collective-permute-start = (bf16[1024,256]{1,0:T(8,128)(2,1)}, bf16[1024,256]{1,0:T(8,128)(2,1)}, u32[]{:S(2)}, u32[]{:S(2)}) collective-permute-start(bf16[1024,256]{1,0:T(8,128)(2,1)} %dress.3), channel_id=1, source_target_pairs={{0,6},{1,7},{2,4},{3,5},{4,2},{5,3},{6,0},{7,1},{8,14},{9,15},{10,... | collective-permute-start | bytes 1572872 | tf_op jit(solution)/shard_map/ppermute | solution.py:24
  21.1 1.8 %cut.1 = bf16[1024,256]{1,0:T(8,128)(2,1)} custom-call(s32[1]{0:T(128)} %bitcast.11.where_ref, bf16[2,1024,1024]{2,1,0:T(8,128)(2,1)} %bitcast.26), custom_call_target="tpu_custom_call" | custom-call | bytes 1048576 | tf_op jit(solution)/shard_map/cut/pallas_call | solution.py:59
  23.6 13.2 %dress.4 = (bf16[1024,256]{1,0:T(8,128)(2,1)}, bf16[1024,256]{1,0:T(8,128)(2,1)}, bf16[1024,256]{1,0:T(8,128)(2,1)}, bf16[1024,256]{1,0:T(8,128)(2,1)}, bf16[102...) custom-call(s32[4]{0:T(128)} %pad_add_fusion.1.where_ref, bf16[2,256,256]{2,1,0:T(8,128)(2,1)} %bitcast.29, ...), custom_call_target="tpu_custom_call" | custom-call | flops 6442450944 | bytes 6291456 | tf_op jit(solution)/shard_map/dress/pallas_call | solution.py:145
  37.6 26.7 %collective-permute-done.3.tile_ref = bf16[1024,256]{1,0:T(8,128)(2,1)S(1)} collective-permute-done((bf16[1024,256]{1,0:T(8,128)(2,1)}, bf16[1024,256]{1,0:T(8,128)(2,1)S(1)}, u32[]{:S(2)}, u32[]{:S(2)}) %collective-permute-start.3) | collective-permute-done | bytes 524320 | tf_op jit(solution)/shard_map/ppermute | solution.py:24
  65.1 2.9 %collective-permute-start.9 = (bf16[2,64,256]{2,1,0:T(8,128)(2,1)S(1)}, bf16[2,64,256]{2,1,0:T(8,128)(2,1)S(1)}, u32[]{:S(2)}, u32[]{:S(2)}) collective-permute-start(bf16[2,64,256]{2,1,0:T(8,128)(2,1)S(1)} %fusion.19), channel_id=1, source_target_pairs={{0,4},{1,5},{2,6},{3,7},{4,0},{5,1},{6,2},{7,3},{8,12},{9,13},{10,... | collective-permute-start | bytes 196616 | tf_op jit(solution)/shard_map/ppermute | solution.py:24
  68.8 23.4 %collective-permute-done.9 = bf16[2,64,256]{2,1,0:T(8,128)(2,1)S(1)} collective-permute-done((bf16[2,64,256]{2,1,0:T(8,128)(2,1)S(1)}, bf16[2,64,256]{2,1,0:T(8,128)(2,1)S(1)}, u32[]{:S(2)}, u32[]{:S(2)}) %collective-permute-start.9) | collective-permute-done | bytes 65568 | tf_op jit(solution)/shard_map/ppermute | solution.py:24
  92.1 2.4 %collective-permute-start.1 = (bf16[1024,256]{1,0:T(8,128)(2,1)}, bf16[1024,256]{1,0:T(8,128)(2,1)}, u32[]{:S(2)}, u32[]{:S(2)}) collective-permute-start(bf16[1024,256]{1,0:T(8,128)(2,1)} %get-tuple-element.27), channel_id=1, source_target_pairs={{0,6},{1,7},{2,4},{3,5},{4,2},{5,3},{6,0},{7,1},{8,14},{9,15},{10,... | collective-permute-start | bytes 1572872 | tf_op jit(solution)/shard_map/ppermute | solution.py:24
  94.6 9.6 %all_gather.7.phi_ref = bf16[2,256,256]{2,1,0:T(8,128)(2,1)} all-gather(bf16[2,64,256]{2,1,0:T(8,128)(2,1)S(1)} %collective-permute-done.9), channel_id=1, replica_groups=mesh['src'=4,'snk'=8] {'src'}, dimensions={1}, use_global_device_ids=true | all-gather | bytes 327680 | tf_op jit(solution)/shard_map/all_gather | solution.py:351
  104.2 5.3 %dress.5.refs_2_ = bf16[1024,256]{1,0:T(8,128)(2,1)} custom-call(s32[1]{0:T(128)} %constant.85.clone.1.where_ref, bf16[2,256,256]{2,1,0:T(8,128)(2,1)} %all_gather.7.phi_ref, bf16[1024,256]{1,0:T(8,128)(2,1)} %copy-done.7), custom_call_target="tpu_custom_call" | custom-call | flops 1073741824 | bytes 1048576 | tf_op jit(solution)/shard_map/dress/pallas_call | solution.py:145
  111.1 2.2 %gather.2.refs_1_ = f32[32,64,256]{2,1,0:T(8,128)S(1)} custom-call(s32[8]{0:T(128)S(1)} %stack.37.sinks_ref, s32[8,16]{1,0:T(8,128)S(1)} %fusion.7.dest_ref, bf16[1024,256]{1,0:T(8,128)(2,1)S(1)} %copy-done.1, bf16[1024,256]{1,0:T(8,128)(2,1)S(1)} %collective-permute-done.2.refs_1_.refs_3_, bf16[1024,256]{1,0:T(8,128)(2,1)S(1)} %collective-permute-done.4.refs_2_.refs_4_, ...), custom_call_target="tpu_custom_call" | custom-call | flops 1572864 | bytes 5242880 | tf_op jit(solution)/shard_map/gather/pallas_call | solution.py:206
  114.1 6.5 %finish.3.refs_1_ = f32[8,64,1024]{2,1,0:T(8,128)S(1)} custom-call(s32[8]{0:T(128)S(1)} %stack.37.sinks_ref, s32[8,16]{1,0:T(8,128)S(1)} %fusion.7.dest_ref, s32[1]{0:T(128)} %bitcast.10.here_ref, bf16[1024,256]{1,0:T(8,128)(2,1)} %get-tuple-element.34.refs_0_, bf16[1024,256]{1,0:T(8,128)(2,1)} %collective-permute-done.8.refs_1_, ...), custom_call_target="tpu_custom_call" | custom-call | flops 4294967296 | bytes 4194304 | tf_op jit(solution)/shard_map/finish/pallas_call | solution.py:301
  120.6 1.5 gather.3.refs_0_
  122.1 2.9 %finish.5 = (f32[4,16,1024]{2,1,0:T(8,128)S(1)}, bf16[4,16,1024]{2,1,0:T(8,128)(2,1)S(1)}, bf16[4,16,1024]{2,1,0:T(8,128)(2,1)S(1)}, bf16[4,16,1024]{2,1,0:T(8,128)(2,1)S(1)}) custom-call(s32[8]{0:T(128)S(1)} %stack.37.sinks_ref, s32[8,16]{1,0:T(8,128)S(1)} %fusion.7.dest_ref, s32[1]{0:T(128)} %bitcast.10.here_ref, f32[32,64,256]{2,1,0:T(8,128)S(1)} %gather.3.refs_0_, ...), custom_call_target="tpu_custom_call" | custom-call | flops 2147483648 | bytes 4194304 | tf_op jit(solution)/shard_map/finish/pallas_call | solution.py:301
  125.0 1.6 %collective-permute-start.19 = (bf16[4,16,1024]{2,1,0:T(8,128)(2,1)S(1)}, bf16[4,16,1024]{2,1,0:T(8,128)(2,1)S(1)}, u32[]{:S(2)}, u32[]{:S(2)}) collective-permute-start(bf16[4,16,1024]{2,1,0:T(8,128)(2,1)S(1)} %get-tuple-element.40), channel_id=1, source_target_pairs={{0,24},{8,16},{16,8},{24,0},{1,25},{9,17},{17,9},{25,1},{2,26},{10... | collective-permute-start | bytes 393224 | tf_op jit(solution)/shard_map/ppermute | solution.py:24
  127.4 1.1 collective-permute-start.21
  128.5 2.9 %finish.4 = (f32[4,16,1024]{2,1,0:T(8,128)S(1)}, bf16[4,16,1024]{2,1,0:T(8,128)(2,1)S(1)}, bf16[4,16,1024]{2,1,0:T(8,128)(2,1)S(1)}, bf16[4,16,1024]{2,1,0:T(8,128)(2,1)S(1)}) custom-call(s32[8]{0:T(128)S(1)} %stack.37.sinks_ref, s32[8,16]{1,0:T(8,128)S(1)} %fusion.7.dest_ref, s32[1]{0:T(128)} %bitcast.10.here_ref, f32[32,64,256]{2,1,0:T(8,128)S(1)} %gather.3.refs_0_, ...), custom_call_target="tpu_custom_call" | custom-call | flops 2147483648 | bytes 4194304 | tf_op jit(solution)/shard_map/finish/pallas_call | solution.py:301
  131.4 1.5 %collective-permute-start.15 = (bf16[4,16,1024]{2,1,0:T(8,128)(2,1)S(1)}, bf16[4,16,1024]{2,1,0:T(8,128)(2,1)S(1)}, u32[]{:S(2)}, u32[]{:S(2)}) collective-permute-start(bf16[4,16,1024]{2,1,0:T(8,128)(2,1)S(1)} %get-tuple-element.36), channel_id=1, source_target_pairs={{0,24},{8,16},{16,8},{24,0},{1,25},{9,17},{17,9},{25,1},{2,26},{10... | collective-permute-start | bytes 393224 | tf_op jit(solution)/shard_map/ppermute | solution.py:24
  133.8 1.1 collective-permute-start.17
  135.0 1.5 collective-permute-start.22
  136.5 6.3 %collective-permute-start.23 = (bf16[2,16,1024]{2,1,0:T(8,128)(2,1)S(1)}, bf16[2,16,1024]{2,1,0:T(8,128)(2,1)S(1)}, u32[]{:S(2)}, u32[]{:S(2)}) collective-permute-start(bf16[2,16,1024]{2,1,0:T(8,128)(2,1)S(1)} %get-tuple-element.44), channel_id=1, source_target_pairs={{0,4},{1,5},{2,6},{3,7},{4,0},{5,1},{6,2},{7,3},{8,12},{9,13},{10,... | collective-permute-start | bytes 196616 | tf_op jit(solution)/shard_map/ppermute | solution.py:24
  142.9 3.4 %collective-permute-start.18 = (bf16[2,16,1024]{2,1,0:T(8,128)(2,1)S(1)}, bf16[2,16,1024]{2,1,0:T(8,128)(2,1)S(1)}, u32[]{:S(2)}, u32[]{:S(2)}) collective-permute-start(bf16[2,16,1024]{2,1,0:T(8,128)(2,1)S(1)} %slice.37), channel_id=1, source_target_pairs={{0,2},{1,3},{2,0},{3,1},{4,6},{5,7},{6,4},{7,5},{8,10},{9,11},{10,... | collective-permute-start | bytes 196616 | tf_op jit(solution)/shard_map/ppermute | solution.py:24
  146.9 1.6 %collective-permute-done.18 = bf16[2,16,1024]{2,1,0:T(8,128)(2,1)S(1)} collective-permute-done((bf16[2,16,1024]{2,1,0:T(8,128)(2,1)S(1)}, bf16[2,16,1024]{2,1,0:T(8,128)(2,1)S(1)}, u32[]{:S(2)}, u32[]{:S(2)}) %collective-permute-start.18) | collective-permute-done | bytes 65568 | tf_op jit(solution)/shard_map/ppermute | solution.py:24
  (64 shorter events, 8.8 us)
Async XLA Ops:
  17.4 50.9 %collective-permute-start = (bf16[1024,256]{1,0:T(8,128)(2,1)}, bf16[1024,256]{1,0:T(8,128)(2,1)}, u32[]{:S(2)}, u32[]{:S(2)}) collective-permute-start(bf16[1024,256]{1,0:T(8,128)(2,1)} %dress.3), channel_id=1, source_target_pairs={{0,6},{1,7},{2,4},{3,5},{4,2},{5,3},{6,0},{7,1},{8,14},{9,15},{10,... | collective-permute-start | bytes 1572872 | tf_op jit(solution)/shard_map/ppermute | solution.py:24
  22.9 41.4 %collective-permute-start.3 = (bf16[1024,256]{1,0:T(8,128)(2,1)}, bf16[1024,256]{1,0:T(8,128)(2,1)S(1)}, u32[]{:S(2)}, u32[]{:S(2)}) collective-permute-start(bf16[1024,256]{1,0:T(8,128)(2,1)} %cut.1), channel_id=1, source_target_pairs={{0,4},{1,5},{2,6},{3,7},{4,0},{5,1},{6,2},{7,3},{8,12},{9,13},{10,... | collective-permute-start | bytes 1572872 | tf_op jit(solution)/shard_map/ppermute | solution.py:24
  36.8 31.4 %collective-permute-start.6 = (bf16[1024,256]{1,0:T(8,128)(2,1)}, bf16[1024,256]{1,0:T(8,128)(2,1)S(1)}, u32[]{:S(2)}, u32[]{:S(2)}) collective-permute-start(bf16[1024,256]{1,0:T(8,128)(2,1)} %get-tuple-element.33), channel_id=1, source_target_pairs={{0,2},{1,3},{2,0},{3,1},{4,6},{5,7},{6,4},{7,5},{8,10},{9,11},{10,... | collective-permute-start | bytes 1572872 | tf_op jit(solution)/shard_map/ppermute | solution.py:24
  65.1 29.4 %collective-permute-start.4 = (bf16[1024,256]{1,0:T(8,128)(2,1)}, bf16[1024,256]{1,0:T(8,128)(2,1)S(1)}, u32[]{:S(2)}, u32[]{:S(2)}) collective-permute-start(bf16[1024,256]{1,0:T(8,128)(2,1)} %get-tuple-element.30), channel_id=1, source_target_pairs={{0,4},{1,5},{2,6},{3,7},{4,0},{5,1},{6,2},{7,3},{8,12},{9,13},{10,... | collective-permute-start | bytes 1572872 | tf_op jit(solution)/shard_map/ppermute | solution.py:24
  65.1 27.0 %collective-permute-start.9 = (bf16[2,64,256]{2,1,0:T(8,128)(2,1)S(1)}, bf16[2,64,256]{2,1,0:T(8,128)(2,1)S(1)}, u32[]{:S(2)}, u32[]{:S(2)}) collective-permute-start(bf16[2,64,256]{2,1,0:T(8,128)(2,1)S(1)} %fusion.19), channel_id=1, source_target_pairs={{0,4},{1,5},{2,6},{3,7},{4,0},{5,1},{6,2},{7,3},{8,12},{9,13},{10,... | collective-permute-start | bytes 196616 | tf_op jit(solution)/shard_map/ppermute | solution.py:24
  68.1 41.4 %collective-permute-start.11 = (bf16[1024,256]{1,0:T(8,128)(2,1)}, bf16[1024,256]{1,0:T(8,128)(2,1)}, u32[]{:S(2)}, u32[]{:S(2)}) collective-permute-start(bf16[1024,256]{1,0:T(8,128)(2,1)} %get-tuple-element.32), channel_id=1, source_target_pairs={{0,2},{1,3},{2,0},{3,1},{4,6},{5,7},{6,4},{7,5},{8,10},{9,11},{10,... | collective-permute-start | bytes 1572872 | tf_op jit(solution)/shard_map/ppermute | solution.py:24
  68.2 41.4 %collective-permute-start.2 = (bf16[1024,256]{1,0:T(8,128)(2,1)}, bf16[1024,256]{1,0:T(8,128)(2,1)S(1)}, u32[]{:S(2)}, u32[]{:S(2)}) collective-permute-start(bf16[1024,256]{1,0:T(8,128)(2,1)} %get-tuple-element.28.refs_0_.refs_2_), channel_id=1, source_target_pairs={{0,1},{1,0},{2,3},{3,2},{4,5},{5,4},{6,7},{7,6},{8,9},{9,8},{10,11... | collective-permute-start | bytes 1572872 | tf_op jit(solution)/shard_map/ppermute | solution.py:24
  68.3 41.8 %collective-permute-start.7 = (bf16[1024,256]{1,0:T(8,128)(2,1)S(1)}, bf16[1024,256]{1,0:T(8,128)(2,1)S(1)}, u32[]{:S(2)}, u32[]{:S(2)}) collective-permute-start(bf16[1024,256]{1,0:T(8,128)(2,1)S(1)} %collective-permute-done.6.refs_4_.refs_6_), channel_id=1, source_target_pairs={{0,1},{1,0},{2,3},{3,2},{4,5},{5,4},{6,7},{7,6},{8,9},{9,8},{10,11... | collective-permute-start | bytes 1572872 | tf_op jit(solution)/shard_map/ppermute | solution.py:24
  92.1 18.0 %collective-permute-start.1 = (bf16[1024,256]{1,0:T(8,128)(2,1)}, bf16[1024,256]{1,0:T(8,128)(2,1)}, u32[]{:S(2)}, u32[]{:S(2)}) collective-permute-start(bf16[1024,256]{1,0:T(8,128)(2,1)} %get-tuple-element.27), channel_id=1, source_target_pairs={{0,6},{1,7},{2,4},{3,5},{4,2},{5,3},{6,0},{7,1},{8,14},{9,15},{10,... | collective-permute-start | bytes 1572872 | tf_op jit(solution)/shard_map/ppermute | solution.py:24
  94.6 16.2 %collective-permute-start.5 = (bf16[1024,256]{1,0:T(8,128)(2,1)S(1)}, bf16[1024,256]{1,0:T(8,128)(2,1)S(1)}, u32[]{:S(2)}, u32[]{:S(2)}) collective-permute-start(bf16[1024,256]{1,0:T(8,128)(2,1)S(1)} %collective-permute-done.4.refs_2_.refs_4_), channel_id=1, source_target_pairs={{0,1},{1,0},{2,3},{3,2},{4,5},{5,4},{6,7},{7,6},{8,9},{9,8},{10,11... | collective-permute-start | bytes 1572872 | tf_op jit(solution)/shard_map/ppermute | solution.py:24
  109.5 3.8 %collective-permute-start.8 = (bf16[1024,256]{1,0:T(8,128)(2,1)}, bf16[1024,256]{1,0:T(8,128)(2,1)}, u32[]{:S(2)}, u32[]{:S(2)}) collective-permute-start(bf16[1024,256]{1,0:T(8,128)(2,1)} %get-tuple-element.34.refs_0_), channel_id=1, source_target_pairs={{0,1},{1,0},{2,3},{3,2},{4,5},{5,4},{6,7},{7,6},{8,9},{9,8},{10,11... | collective-permute-start | bytes 1572872 | tf_op jit(solution)/shard_map/ppermute | solution.py:24
  109.6 4.5 %collective-permute-start.10 = (bf16[1024,256]{1,0:T(8,128)(2,1)}, bf16[1024,256]{1,0:T(8,128)(2,1)}, u32[]{:S(2)}, u32[]{:S(2)}) collective-permute-start(bf16[1024,256]{1,0:T(8,128)(2,1)} %dress.5.refs_2_), channel_id=1, source_target_pairs={{0,1},{1,0},{2,3},{3,2},{4,5},{5,4},{6,7},{7,6},{8,9},{9,8},{10,11... | collective-permute-start | bytes 1572872 | tf_op jit(solution)/shard_map/ppermute | solution.py:24
  110.1 4.0 %collective-permute-start.13 = (bf16[1024,256]{1,0:T(8,128)(2,1)}, bf16[1024,256]{1,0:T(8,128)(2,1)}, u32[]{:S(2)}, u32[]{:S(2)}) collective-permute-start(bf16[1024,256]{1,0:T(8,128)(2,1)} %collective-permute-done.refs_6_), channel_id=1, source_target_pairs={{0,1},{1,0},{2,3},{3,2},{4,5},{5,4},{6,7},{7,6},{8,9},{9,8},{10,11... | collective-permute-start | bytes 1572872 | tf_op jit(solution)/shard_map/ppermute | solution.py:24
  110.2 3.9 %collective-permute-start.12 = (bf16[1024,256]{1,0:T(8,128)(2,1)}, bf16[1024,256]{1,0:T(8,128)(2,1)}, u32[]{:S(2)}, u32[]{:S(2)}) collective-permute-start(bf16[1024,256]{1,0:T(8,128)(2,1)} %collective-permute-done.11.refs_4_), channel_id=1, source_target_pairs={{0,1},{1,0},{2,3},{3,2},{4,5},{5,4},{6,7},{7,6},{8,9},{9,8},{10,11... | collective-permute-start | bytes 1572872 | tf_op jit(solution)/shard_map/ppermute | solution.py:24
  110.8 11.3 %collective-permute-start.14 = (bf16[1024,256]{1,0:T(8,128)(2,1)}, bf16[1024,256]{1,0:T(8,128)(2,1)}, u32[]{:S(2)}, u32[]{:S(2)}) collective-permute-start(bf16[1024,256]{1,0:T(8,128)(2,1)} %collective-permute-done.1.refs_0_.refs_8_), channel_id=1, source_target_pairs={{0,1},{1,0},{2,3},{3,2},{4,5},{5,4},{6,7},{7,6},{8,9},{9,8},{10,11... | collective-permute-start | bytes 1572872 | tf_op jit(solution)/shard_map/ppermute | solution.py:24
  125.0 8.8 %collective-permute-start.19 = (bf16[4,16,1024]{2,1,0:T(8,128)(2,1)S(1)}, bf16[4,16,1024]{2,1,0:T(8,128)(2,1)S(1)}, u32[]{:S(2)}, u32[]{:S(2)}) collective-permute-start(bf16[4,16,1024]{2,1,0:T(8,128)(2,1)S(1)} %get-tuple-element.40), channel_id=1, source_target_pairs={{0,24},{8,16},{16,8},{24,0},{1,25},{9,17},{17,9},{25,1},{2,26},{10... | collective-permute-start | bytes 393224 | tf_op jit(solution)/shard_map/ppermute | solution.py:24
  126.5 8.4 %collective-permute-start.20 = (bf16[4,16,1024]{2,1,0:T(8,128)(2,1)S(1)}, bf16[4,16,1024]{2,1,0:T(8,128)(2,1)S(1)}, u32[]{:S(2)}, u32[]{:S(2)}) collective-permute-start(bf16[4,16,1024]{2,1,0:T(8,128)(2,1)S(1)} %get-tuple-element.41), channel_id=1, source_target_pairs={{0,16},{8,24},{16,0},{24,8},{1,17},{9,25},{17,1},{25,9},{2,18},{10... | collective-permute-start | bytes 393224 | tf_op jit(solution)/shard_map/ppermute | solution.py:24
  127.4 7.6 %collective-permute-start.21 = (bf16[4,16,1024]{2,1,0:T(8,128)(2,1)S(1)}, bf16[4,16,1024]{2,1,0:T(8,128)(2,1)S(1)}, u32[]{:S(2)}, u32[]{:S(2)}) collective-permute-start(bf16[4,16,1024]{2,1,0:T(8,128)(2,1)S(1)} %get-tuple-element.42), channel_id=1, source_target_pairs={{0,8},{8,0},{16,24},{24,16},{1,9},{9,1},{17,25},{25,17},{2,10},{10... | collective-permute-start | bytes 393224 | tf_op jit(solution)/shard_map/ppermute | solution.py:24
  131.4 11.4 %collective-permute-start.15 = (bf16[4,16,1024]{2,1,0:T(8,128)(2,1)S(1)}, bf16[4,16,1024]{2,1,0:T(8,128)(2,1)S(1)}, u32[]{:S(2)}, u32[]{:S(2)}) collective-permute-start(bf16[4,16,1024]{2,1,0:T(8,128)(2,1)S(1)} %get-tuple-element.36), channel_id=1, source_target_pairs={{0,24},{8,16},{16,8},{24,0},{1,25},{9,17},{17,9},{25,1},{2,26},{10... | collective-permute-start | bytes 393224 | tf_op jit(solution)/shard_map/ppermute | solution.py:24
  132.9 9.9 %collective-permute-start.16 = (bf16[4,16,1024]{2,1,0:T(8,128)(2,1)S(1)}, bf16[4,16,1024]{2,1,0:T(8,128)(2,1)S(1)}, u32[]{:S(2)}, u32[]{:S(2)}) collective-permute-start(bf16[4,16,1024]{2,1,0:T(8,128)(2,1)S(1)} %get-tuple-element.37), channel_id=1, source_target_pairs={{0,16},{8,24},{16,0},{24,8},{1,17},{9,25},{17,1},{25,9},{2,18},{10... | collective-permute-start | bytes 393224 | tf_op jit(solution)/shard_map/ppermute | solution.py:24
  133.8 9.0 %collective-permute-start.17 = (bf16[4,16,1024]{2,1,0:T(8,128)(2,1)S(1)}, bf16[4,16,1024]{2,1,0:T(8,128)(2,1)S(1)}, u32[]{:S(2)}, u32[]{:S(2)}) collective-permute-start(bf16[4,16,1024]{2,1,0:T(8,128)(2,1)S(1)} %get-tuple-element.38), channel_id=1, source_target_pairs={{0,8},{8,0},{16,24},{24,16},{1,9},{9,1},{17,25},{25,17},{2,10},{10... | collective-permute-start | bytes 393224 | tf_op jit(solution)/shard_map/ppermute | solution.py:24
  135.0 11.2 %collective-permute-start.22 = (bf16[2,16,1024]{2,1,0:T(8,128)(2,1)S(1)}, bf16[2,16,1024]{2,1,0:T(8,128)(2,1)S(1)}, u32[]{:S(2)}, u32[]{:S(2)}) collective-permute-start(bf16[2,16,1024]{2,1,0:T(8,128)(2,1)S(1)} %get-tuple-element.43), channel_id=1, source_target_pairs={{0,6},{1,7},{2,4},{3,5},{4,2},{5,3},{6,0},{7,1},{8,14},{9,15},{10,... | collective-permute-start | bytes 196616 | tf_op jit(solution)/shard_map/ppermute | solution.py:24
  136.5 10.4 %collective-permute-start.23 = (bf16[2,16,1024]{2,1,0:T(8,128)(2,1)S(1)}, bf16[2,16,1024]{2,1,0:T(8,128)(2,1)S(1)}, u32[]{:S(2)}, u32[]{:S(2)}) collective-permute-start(bf16[2,16,1024]{2,1,0:T(8,128)(2,1)S(1)} %get-tuple-element.44), channel_id=1, source_target_pairs={{0,4},{1,5},{2,6},{3,7},{4,0},{5,1},{6,2},{7,3},{8,12},{9,13},{10,... | collective-permute-start | bytes 196616 | tf_op jit(solution)/shard_map/ppermute | solution.py:24
  142.9 5.6 %collective-permute-start.18 = (bf16[2,16,1024]{2,1,0:T(8,128)(2,1)S(1)}, bf16[2,16,1024]{2,1,0:T(8,128)(2,1)S(1)}, u32[]{:S(2)}, u32[]{:S(2)}) collective-permute-start(bf16[2,16,1024]{2,1,0:T(8,128)(2,1)S(1)} %slice.37), channel_id=1, source_target_pairs={{0,2},{1,3},{2,0},{3,1},{4,6},{5,7},{6,4},{7,5},{8,10},{9,11},{10,... | collective-permute-start | bytes 196616 | tf_op jit(solution)/shard_map/ppermute | solution.py:24
  (8 other events, 75.9 us)
